TPU v7x, 32 devices: a whole 2x2x4 slice. The times are simulated.
32 devices in a mesh: px: 2 (over core), pz: 16 (over z, y, x).
Axes of the slice: x: 2, y: 2, z: 4, core: 2. Of those that a mesh axis runs over, the one named last changes fastest.
Arguments:
- velocity: float32 [3, 256, 32, 256], P(None, 'pz', None, 'px'), may hold values from -8 to 8, as said below
- filter_inverse: float32 [256, 256], replicated, may hold values from 0 to 2, as said below
- filter_block: int32 [256], replicated, may hold values from 0 to 7, never falling along the last dimension, each value on 1 to 128 neighbouring positions
- plane_bin: int32 [256], replicated, may hold values from 0 to 63, never falling along the last dimension, each value on 1 to 16 neighbouring positions
Outputs:
- leonard: float32 [6, 256, 32, 256], P(None, 'pz', None, 'px')
- viscosity: float32 [256, 32, 256], P('pz', None, 'px')
- coefficient: float32 [256], replicated
Inputs may be any that keep to these rules, and one draw needn't show every extreme that they name: `velocity`: each component is a rough random field. `filter_inverse`: entries are positive. `filter_block`: never falls along the planes; each of the 8 blocks holds 1 to 128 consecutive planes, one exactly 128. `plane_bin`: never falls along the planes; each of the 64 bins holds 1 to 16 consecutive planes, one exactly 16.
All inputs are finite; a program needn't handle non-finite values.
Results may differ from a plain program's by a relative error of at most 0.0003.
Values sent between devices are 32-bit elements; how exact they have to be, the bound alone decides.
A program may use at most 128 MiB of HBM per device.

v0:
```python
import functools

import jax
import jax.numpy as jnp
from jax import lax
from jax.experimental import pallas as pl
from jax.experimental.pallas import tpu as pltpu
from jax.sharding import PartitionSpec as P

NBIN = 64
MESH = pl.DeviceIdType.MESH
PAIRS = ((0, 0), (1, 1), (2, 2), (0, 1), (0, 2), (1, 2))


def tensor_norm(s):
    diag = s[0] * s[0] + s[1] * s[1] + s[2] * s[2]
    off = s[3] * s[3] + s[4] * s[4] + s[5] * s[5]
    return jnp.sqrt(2.0 * diag + 4.0 * off)


def strain_of(dx, dy, dz):
    return [
        dx[0] * 0.5,
        dy[1] * 0.5,
        dz[2] * 0.5,
        0.25 * (dy[0] + dx[1]),
        0.25 * (dz[0] + dx[2]),
        0.25 * (dz[1] + dy[2]),
    ]


def fill_from_blocks(dims, ext, own, right, left):
    n, win, lp, nx = dims
    lane = lax.broadcasted_iota(jnp.int32, (lp, nx), 1)
    from_right = lane < nx // 2

    @pl.loop(0, n)
    def _(p):
        rows = pl.ds(pl.multiple_of(8 + p * lp, 8), lp)
        for c in range(3):
            for z in range(win):
                ext[c, z, rows, 0:nx] = own[p, c, z]
                ext[c, z, rows, nx : 2 * nx] = jnp.where(from_right, right[p, c, z], left[p, c, z])


def fill_from_halves(dims, ext, core, own, own_edge, other, other_edge):
    n, win, lp, nx = dims
    half = win - 2
    here = core[0]

    def place(source, edges, p, c, w, at, z):
        rows = pl.ds(pl.multiple_of(8 + p * lp, 8), lp)
        ext[c, z, rows, 0:nx] = source[p, w, c * lp : (c + 1) * lp, :]
        for r in range(lp // 8):
            shift = 2 * nx - 2 - 4 * (r * 3 * half + at)
            part = pltpu.roll(edges[p], lax.rem(shift, nx), 1)
            ext[c, z, pl.ds(pl.multiple_of(8 + p * lp + 8 * r, 8), 8), nx : 2 * nx] = part

    @pl.loop(0, n)
    def _(p):
        for c in range(3):
            for w in range(half):
                place(own, own_edge, p, c, w, w * 3 + c, w + 2 * here)
            for w in range(2):
                at = (w + (half - 2) * here) * 3 + c
                place(other, other_edge, p, c, w, at, w + half * (1 - here))


def column_kernel(dims, fill, sources, *refs):
    n, win, lp, nx = dims
    blocks, refs = refs[:sources], refs[sources:]
    weights, onehot, back, ext, bhi, blo, filt, lms, mms, whi, wlo = refs
    zs = win - 4
    ny = n * lp
    lanes = 2 * nx
    heavy = weights[...].astype(jnp.bfloat16)
    whi[...] = heavy
    wlo[...] = (weights[...] - heavy.astype(jnp.float32)).astype(jnp.bfloat16)

    zero = jnp.zeros((8, lanes), jnp.float32)
    for c in range(3):
        for z in range(win):
            ext[c, z, 0:8, :] = zero
            ext[c, z, ny + 8 : ny + 16, :] = zero
    fill(dims, ext, *blocks)

    @pl.loop(0, n)
    def _(p):
        base = pl.multiple_of(p * lp, 8)
        u = [[ext[c, z, pl.ds(base + 8, lp), :] for z in range(win)] for c in range(3)]
        boxes = [[None] * 21 for _ in range(zs)]
        for z in range(1, win - 1):
            v = [u[c][z] for c in range(3)]
            dx, dy, dz = [], [], []
            for c in range(3):
                dx.append(pltpu.roll(v[c], lanes - 1, 1) - pltpu.roll(v[c], 1, 1))
                tall = ext[c, z, pl.ds(base, lp + 16), :]
                dy.append(tall[9 : 9 + lp] - tall[7 : 7 + lp])
                dz.append(u[c][z + 1] - u[c][z - 1])
            s = strain_of(dx, dy, dz)
            mag = tensor_norm(s)
            fields = v + s + [v[i] * v[j] for i, j in PAIRS] + [mag * t for t in s]
            for o in range(zs):
                step = z - (o + 2)
                if -1 <= step <= 1:
                    for k in range(21):
                        term = fields[k] if step else 2.0 * fields[k]
                        boxes[o][k] = term if boxes[o][k] is None else boxes[o][k] + term
        for o in range(zs):
            for k in range(21):
                f = boxes[o][k]
                box = (pltpu.roll(f, 1, 1) + pltpu.roll(f, lanes - 1, 1) + 2.0 * f)[:, :nx] * 0.0625
                high = box.astype(jnp.bfloat16)
                cols = slice(o * nx, (o + 1) * nx)
                bhi[k, pl.ds(base, lp), cols] = high
                blo[k, pl.ds(base, lp), cols] = (box - high.astype(jnp.float32)).astype(jnp.bfloat16)

    @pl.loop(0, 21)
    def _(k):
        dot = functools.partial(jnp.dot, preferred_element_type=jnp.float32)
        filt[k] = dot(whi[...], bhi[k]) + (dot(whi[...], blo[k]) + dot(wlo[...], bhi[k]))

    @pl.loop(0, n)
    def _(p):
        base = pl.multiple_of(p * lp, 8)
        lm_total = jnp.zeros((lp, nx), jnp.float32)
        mm_total = jnp.zeros((lp, nx), jnp.float32)
        for o in range(zs):
            g = [filt[k, pl.ds(base, lp), o * nx : (o + 1) * nx] for k in range(21)]
            fmag = 4.0 * tensor_norm(g[3:9])
            for q, (i, j) in enumerate(PAIRS):
                leonard = g[9 + q] - g[i] * g[j]
                model = g[15 + q] - fmag * g[3 + q]
                weighted = model if q < 3 else 2.0 * model
                lm_total += leonard * weighted
                mm_total += model * weighted
                back[p, (q * zs + o) * lp : (q * zs + o + 1) * lp, :] = leonard
        lms[pl.ds(base, lp), :] = lm_total
        mms[pl.ds(base, lp), :] = mm_total

    ones = jnp.ones((8, nx), jnp.float32)
    exact = functools.partial(
        lax.dot_general, preferred_element_type=jnp.float32, precision=lax.Precision.HIGHEST
    )
    totals = []
    for part in (lms, mms):
        planes = exact(ones, part[...], (((1,), (1,)), ((), ())))
        totals.append(exact(planes, onehot[...], (((1,), (0,)), ((), ()))))
    row = lax.broadcasted_iota(jnp.int32, (8, onehot.shape[1]), 0)
    tile = jnp.where(row < 4, totals[0], totals[1])
    for p in range(n):
        back[p, 6 * zs * lp :, :] = tile


def greet_all(m, n):
    me = lax.axis_index("px") * n + lax.axis_index("pz")
    barrier = pltpu.get_barrier_semaphore()

    @pl.loop(1, m * n)
    def _(step):
        peer = lax.rem(me + step, m * n)
        pl.semaphore_signal(barrier, inc=1, device_id=(peer // n, lax.rem(peer, n)), device_id_type=MESH)

    pl.semaphore_wait(barrier, m * n - 1)


def edge_kernel(dims, main, edge):
    half, lp, nx = dims
    lane = lax.broadcasted_iota(jnp.int32, (8, nx), 1)

    @pl.loop(0, edge.shape[0])
    def _(i):
        tile = jnp.zeros((8, nx), jnp.float32)
        for r in range(lp // 8):
            for w in range(half):
                for c in range(3):
                    at = 4 * ((r * half + w) * 3 + c)
                    cells = main[i * half + w, c * lp + r * 8 : c * lp + r * 8 + 8, :]
                    tile = jnp.where((lane >= at) & (lane < at + 4), pltpu.roll(cells, (at + 2) % nx, 1), tile)
        edge[i] = tile


def outward_kernel(dims, main, edge, own, own_edge, other, other_edge, main_out, main_in, edge_out, edge_in, pass_out, pass_in):
    n, half, lp = dims
    a, s = lax.axis_index("px"), lax.axis_index("pz")
    greet_all(2, n)

    def send(source, t, parity, dst, out_sem, in_sem):
        core, chip = lax.rem(t, 2), 2 * (t // 2) + parity
        itself = (core == a) & (chip == s)
        copy = pltpu.make_async_remote_copy(
            source, dst, out_sem.at[t], in_sem.at[s], device_id=(core, chip), device_id_type=MESH
        )
        return itself, copy, pltpu.make_async_copy(source, dst, in_sem.at[s])

    def sends(t):
        return (
            send(edge.at[t // 2 + lax.rem(t, 2)], t, 1 - a, own_edge.at[s], edge_out, edge_in),
            send(main.at[pl.ds((t // 2 + lax.rem(t, 2)) * half, half)], t, a, own.at[s], main_out, main_in),
        )

    @pl.loop(0, n)
    def _(i):
        for itself, copy, here in sends(lax.rem(s + i, n)):
            pl.when(itself)(here.start)
            pl.when(jnp.logical_not(itself))(copy.start)

    first = (1 - a) * (half - 2)

    def passes(p):
        return [
            pltpu.make_async_remote_copy(
                src, dst, pass_out.at[j, p], pass_in.at[j, p],
                device_id=(1 - a, s), device_id_type=MESH,
            )
            for j, (src, dst) in enumerate(
                ((own.at[p, pl.ds(first, 2)], other.at[p]), (own_edge.at[p], other_edge.at[p]))
            )
        ]

    @pl.loop(0, n)
    def _(i):
        p = lax.rem(s + n - i, n)
        pltpu.make_async_copy(main.at[0:half], own.at[p], main_in.at[p]).wait()
        pltpu.make_async_copy(edge.at[0], own_edge.at[p], edge_in.at[p]).wait()
        for copy in passes(p):
            copy.start()

    @pl.loop(0, n)
    def _(p):
        for copy in passes(p):
            copy.wait()
        for itself, copy, here in sends(p):
            pl.when(jnp.logical_not(itself))(copy.wait_send)


def return_kernel(n, back, velocity, home, out, beside, near, back_out, back_in, halo_out, halo_in):
    _, lp, nz, nx = velocity.shape
    a, s = lax.axis_index("px"), lax.axis_index("pz")
    greet_all(2, n)
    slot = 2 * (s // 2) + a
    parity = lax.rem(s, 2)
    remote = functools.partial(pltpu.make_async_remote_copy, device_id_type=MESH)
    halos = [
        remote(velocity, beside, halo_out.at[0], halo_in.at[0], device_id=(1 - a, s)),
        remote(velocity.at[:, lp - 1], near.at[0], halo_out.at[1], halo_in.at[1], device_id=(a, lax.rem(s + 1, n))),
        remote(velocity.at[:, 0], near.at[1], halo_out.at[2], halo_in.at[2], device_id=(a, lax.rem(s + n - 1, n))),
    ]
    for copy in halos:
        copy.start()

    def send(p):
        itself = (parity == a) & (p == s)
        copy = remote(back.at[p], home.at[slot], back_out.at[p], back_in.at[slot], device_id=(parity, p))
        return itself, copy, pltpu.make_async_copy(back.at[p], home.at[slot], back_in.at[slot])

    @pl.loop(0, n)
    def _(i):
        itself, copy, here = send(lax.rem(s + i, n))
        pl.when(itself)(here.start)
        pl.when(jnp.logical_not(itself))(copy.start)

    for copy in halos:
        copy.wait()
    lane = lax.broadcasted_iota(jnp.int32, (nz, nx), 1)
    has_below = (s > 0).astype(jnp.float32)
    has_above = (s < n - 1).astype(jnp.float32)

    def plane(y, ups, downs):
        dx, dy, dz = [], [], []
        for c in range(3):
            v, side = velocity[c, y], beside[c, y]
            ahead = jnp.where(lane == nx - 1, pltpu.roll(side, nx - 1, 1), pltpu.roll(v, nx - 1, 1))
            behind = jnp.where(lane == 0, pltpu.roll(side, 1, 1), pltpu.roll(v, 1, 1))
            dx.append(ahead - behind)
            dz.append(pltpu.roll(v, nz - 1, 0) - pltpu.roll(v, 1, 0))
            dy.append(ups[c] - downs[c])
        out[y] = tensor_norm(strain_of(dx, dy, dz))

    line = [near[0, c] * has_below for c in range(3)]
    plane(0, [velocity[c, 1] for c in range(3)], line)
    line = [near[1, c] * has_above for c in range(3)]
    plane(lp - 1, line, [velocity[c, lp - 2] for c in range(3)])

    @pl.loop(1, lp - 1)
    def _(y):
        plane(y, [velocity[c, y + 1] for c in range(3)], [velocity[c, y - 1] for c in range(3)])

    @pl.loop(0, n)
    def _(p):
        pltpu.make_async_copy(back.at[0], home.at[p], back_in.at[p]).wait()
        itself, copy, here = send(p)
        pl.when(jnp.logical_not(itself))(copy.wait_send)


def magnitude_kernel(centre, right, left, below, above, out):
    _, lp, nz, nx = centre.shape
    lane = lax.broadcasted_iota(jnp.int32, (nz, nx), 1)
    for y in range(lp):
        v = [centre[c, y] for c in range(3)]
        dx, dy, dz = [], [], []
        for c in range(3):
            ahead = jnp.where(lane == nx - 1, pltpu.roll(right[c, y], nx - 1, 1), pltpu.roll(v[c], nx - 1, 1))
            behind = jnp.where(lane == 0, pltpu.roll(left[c, y], 1, 1), pltpu.roll(v[c], 1, 1))
            dx.append(ahead - behind)
            dz.append(pltpu.roll(v[c], nz - 1, 0) - pltpu.roll(v[c], 1, 0))
            up = centre[c, y + 1] if y + 1 < lp else above[c, 0]
            down = centre[c, y - 1] if y else below[c, 0]
            dy.append(up - down)
        out[y] = tensor_norm(strain_of(dx, dy, dz))


def local(velocity, filter_inverse, filter_block, plane_bin):
    _, lp, nz, nx = velocity.shape
    n = lax.axis_size("pz")
    m = lax.axis_size("px")
    ny, zs = n * lp, nz // n
    win = zs + 4
    half = zs + 2
    shared = m == 2 and n % 2 == 0 and n > 2 and half == 2 * zs and 12 * half * (lp // 8) <= nx
    core = lax.axis_index("px")

    same = (filter_block[:, None] == filter_block[None, :]).astype(jnp.float32)
    masked = filter_inverse * same
    weights = masked / jnp.sum(masked, axis=1, keepdims=True)
    onehot = (plane_bin[:, None] == jnp.arange(nx, dtype=jnp.int32)[None, :]).astype(jnp.float32)

    if shared:
        turned = jnp.transpose(velocity, (2, 0, 1, 3)).reshape(nz, 3 * lp, nx)
        main = jnp.concatenate([turned[-2:], turned, turned[:2]], axis=0)
        edge = pl.pallas_call(
            functools.partial(edge_kernel, (half, lp, nx)),
            out_shape=jax.ShapeDtypeStruct((n // 2 + 1, 8, nx), jnp.float32),
        )(main)
        own, own_edge, other, other_edge = pl.pallas_call(
            functools.partial(outward_kernel, (n, half, lp)),
            out_shape=(
                jax.ShapeDtypeStruct((n, half, 3 * lp, nx), jnp.float32),
                jax.ShapeDtypeStruct((n, 8, nx), jnp.float32),
                jax.ShapeDtypeStruct((n, 2, 3 * lp, nx), jnp.float32),
                jax.ShapeDtypeStruct((n, 8, nx), jnp.float32),
            ),
            in_specs=[pl.BlockSpec(memory_space=pltpu.VMEM)] * 2,
            out_specs=(pl.BlockSpec(memory_space=pltpu.VMEM),) * 4,
            scratch_shapes=[pltpu.SemaphoreType.DMA((n,))] * 4 + [pltpu.SemaphoreType.DMA((2, n))] * 2,
            compiler_params=pltpu.CompilerParams(collective_id=0, has_side_effects=True),
        )(main, edge)
        fill, blocks = fill_from_halves, (core.astype(jnp.int32).reshape(1), own, own_edge, other, other_edge)
        specs = [pl.BlockSpec(memory_space=pltpu.SMEM)] + [pl.BlockSpec(memory_space=pltpu.VMEM)] * 4
    else:
        right = lax.ppermute(velocity, "px", [((i + 1) % m, i) for i in range(m)])
        left = right if m == 2 else lax.ppermute(velocity, "px", [(i, (i + 1) % m) for i in range(m)])
        below = lax.ppermute(velocity[:, -1:], "pz", [(i, i + 1) for i in range(n - 1)])
        above = lax.ppermute(velocity[:, :1], "pz", [(i + 1, i) for i in range(n - 1)])
        magnitude = pl.pallas_call(
            magnitude_kernel,
            out_shape=jax.ShapeDtypeStruct((lp, nz, nx), jnp.float32),
            cost_estimate=pl.CostEstimate(flops=60 * lp * nz * nx, bytes_accessed=40 * lp * nz * nx, transcendentals=0),
        )(velocity, right, left, below, above)
        turned = jnp.transpose(velocity, (0, 2, 1, 3))
        turned = jnp.concatenate([turned[:, -2:], turned, turned[:, :2]], axis=1)
        sent = jnp.stack([turned[:, t * zs : t * zs + win] for t in range(n)])
        own = lax.all_to_all(sent, "pz", split_axis=0, concat_axis=0, tiled=True)
        ahead = lax.ppermute(own, "px", [((i + 1) % m, i) for i in range(m)])
        behind = lax.ppermute(own, "px", [(i, (i + 1) % m) for i in range(m)])
        fill, blocks = fill_from_blocks, (own, ahead, behind)
        specs = [pl.BlockSpec(memory_space=pltpu.VMEM)] * 3

    rows = 6 * zs * lp
    back = pl.pallas_call(
        functools.partial(column_kernel, (n, win, lp, nx), fill, len(blocks)),
        out_shape=jax.ShapeDtypeStruct((n, rows + 8, nx), jnp.float32),
        in_specs=specs + [pl.BlockSpec(memory_space=pltpu.VMEM)] * 2,
        out_specs=pl.BlockSpec(memory_space=pltpu.VMEM),
        scratch_shapes=[
            pltpu.VMEM((3, win, ny + 16, 2 * nx), jnp.float32),
            pltpu.VMEM((21, ny, zs * nx), jnp.bfloat16),
            pltpu.VMEM((21, ny, zs * nx), jnp.bfloat16),
            pltpu.VMEM((21, ny, zs * nx), jnp.float32),
            pltpu.VMEM((ny, nx), jnp.float32),
            pltpu.VMEM((ny, nx), jnp.float32),
            pltpu.VMEM((ny, ny), jnp.bfloat16),
            pltpu.VMEM((ny, ny), jnp.bfloat16),
        ],
        compiler_params=pltpu.CompilerParams(vmem_limit_bytes=60 * 1024 * 1024),
    )(*blocks, weights, onehot)

    if shared:
        home, magnitude = pl.pallas_call(
            functools.partial(return_kernel, n),
            out_shape=(
                jax.ShapeDtypeStruct(back.shape, jnp.float32),
                jax.ShapeDtypeStruct((lp, nz, nx), jnp.float32),
            ),
            in_specs=[pl.BlockSpec(memory_space=pltpu.VMEM)] * 2,
            out_specs=(pl.BlockSpec(memory_space=pltpu.VMEM),) * 2,
            scratch_shapes=[
                pltpu.VMEM((3, lp, nz, nx), jnp.float32),
                pltpu.VMEM((2, 3, nz, nx), jnp.float32),
                pltpu.SemaphoreType.DMA((n,)),
                pltpu.SemaphoreType.DMA((n,)),
                pltpu.SemaphoreType.DMA((3,)),
                pltpu.SemaphoreType.DMA((3,)),
            ],
            compiler_params=pltpu.CompilerParams(collective_id=1, has_side_effects=True),
        )(back, velocity)
        totals = jnp.sum(home[:, rows:], axis=0)
        totals = totals + lax.ppermute(totals, "px", [(0, 1), (1, 0)])
    else:
        home = lax.all_to_all(back, "pz", split_axis=0, concat_axis=0, tiled=True)
        totals = lax.psum(jnp.sum(home[:, rows:], axis=0), "px")
    stress = home[:, :rows].reshape(n, 6, zs, lp, nx)
    leonard = jnp.transpose(stress, (1, 3, 0, 2, 4)).reshape(6, lp, nz, nx)
    numer, denom = totals[0, :NBIN], totals[4, :NBIN]
    cells = nx * m * nz
    per_bin = numer / jnp.maximum(denom, jnp.float32(cells))
    coefficient = jnp.dot(onehot[:, :NBIN], per_bin, precision=lax.Precision.HIGHEST)
    local_coef = lax.dynamic_slice_in_dim(coefficient, lax.axis_index("pz") * lp, lp, 0)
    viscosity = local_coef[:, None, None] * magnitude
    return (leonard, viscosity, coefficient)


def solution(mesh):
    return jax.shard_map(
        local,
        mesh=mesh,
        in_specs=(P(None, "pz", None, "px"), P(), P(), P()),
        out_specs=(P(None, "pz", None, "px"), P("pz", None, "px"), P()),
        check_vma=False,
    )
```

profile of v0, /device:TPU:31, one launch (start us, length us, event | category | flops | bytes accessed | tf_op | source)
XLA Modules:
  0.0 128.9 jit_solution(11919600758105364836)
XLA Ops:
  0.6 0.0 copy-start.3
  0.6 0.0 copy-start.2
  0.7 0.0 copy-start
  0.7 1.1 fusion.10
  1.8 1.6 %copy.8 = f32[32,3,16,128]{3,2,1,0:T(8,128)S(1)} copy(f32[32,3,16,128]{3,0,2,1:T(8,128)} %bitcast.16) | data formatting | bytes 1572864 | tf_op jit(solution)/shard_map/transpose | solution.py:329
  3.4 0.0 copy-done.3
  3.4 0.8 iota_compare_fusion
  4.2 0.0 copy-done.2
  4.2 0.0 copy-done
  4.2 0.2 fusion.1
  4.4 0.8 fusion.refs_5_
  5.2 1.0 pad_maximum_fusion.main
  6.2 2.6 %shard_map.67.edge = f32[9,8,128]{2,1,0:T(8,128)} custom-call(f32[36,48,128]{2,1,0:T(8,128)} %pad_maximum_fusion.main), custom_call_target="tpu_custom_call" | custom-call | tf_op jit(solution)/shard_map/pallas_call | solution.py:331
  8.8 45.1 %shard_map.68 = (f32[16,4,48,128]{3,2,1,0:T(8,128)}, f32[16,8,128]{2,1,0:T(8,128)}, f32[16,2,48,128]{3,2,1,0:T(8,128)}, f32[16,8,128]{2,1,0:T(8,128)}) custom-call(f32[36,48,128]{2,1,0:T(8,128)} %pad_maximum_fusion.main, f32[9,8,128]{2,1,0:T(8,128)} %shard_map.67.edge), custom_call_target="tpu_custom_call" | custom-call | tf_op jit(solution)/shard_map/pallas_call | solution.py:335
  53.9 21.3 %shard_map.69.back = f32[16,200,128]{2,1,0:T(8,128)} custom-call(s32[1]{0:T(128)} %bitcast.refs_0_, f32[16,4,48,128]{3,2,1,0:T(8,128)} %get-tuple-element.9.refs_1_, f32[16,8,128]{2,1,0:T(8,128)} %get-tuple-element.10.refs_2_, f32[16,2,48,128]{3,2,1,0:T(8,128)} %get-tuple-element.11.refs_3_, f32[16,8,128]{2,1,0:T(8,128)} %get-tuple-element.12.refs_4_, ...), custom_call_target="tpu_custom_call" | custom-call | tf_op jit(solution)/shard_map/pallas_call | solution.py:370
  75.2 47.5 %shard_map.70 = (f32[16,200,128]{2,1,0:T(8,128)}, f32[16,32,128]{2,1,0:T(8,128)}) custom-call(f32[16,200,128]{2,1,0:T(8,128)} %shard_map.69.back, f32[3,16,32,128]{3,2,1,0:T(8,128)} %velocity.1), custom_call_target="tpu_custom_call" | custom-call | tf_op jit(solution)/shard_map/pallas_call | solution.py:389
  122.7 0.9 slice_reduce_fusion
  123.6 0.7 collective-permute-start
  124.3 1.5 %slice.31 = f32[16,192,128]{2,1,0:T(8,128)S(1)} slice(f32[16,200,128]{2,1,0:T(8,128)} %get-tuple-element.13), slice={[0:16], [0:192], [0:128]} | slice | bytes 3145728 | tf_op jit(solution)/shard_map/slice | solution.py:412
  125.8 0.0 copy-start.1
  125.8 2.0 %copy.10 = f32[6,16,16,2,128]{4,3,2,1,0:T(2,128)} copy(f32[6,16,16,2,128]{4,1,3,0,2:T(8,128)S(1)} %bitcast.14) | data formatting | bytes 3145728 | tf_op jit(solution)/shard_map/transpose | solution.py:413
  127.8 0.0 collective-permute-done
  127.8 0.1 fusion.2
  128.0 0.0 copy-start.4
  128.0 0.1 dynamic_slice.3
  128.1 0.0 copy-done.1
  128.1 0.8 broadcast_multiply_fusion
  128.9 0.0 copy-done.4
  (3 shorter events, 0.0 us)
Async XLA Ops:
  0.6 2.8 %copy-start.3 = (s32[256]{0:T(256)S(1)}, s32[256]{0:T(256)}, u32[]{:S(2)}) copy-start(s32[256]{0:T(256)} %param.7) | copy-start | bytes 3076
  0.6 3.5 %copy-start.2 = (s32[256]{0:T(256)S(1)}, s32[256]{0:T(256)}, u32[]{:S(2)}) copy-start(s32[256]{0:T(256)} %param.6) | copy-start | bytes 3076
  0.7 3.5 %copy-start = (f32[256,256]{1,0:T(8,128)S(1)}, f32[256,256]{1,0:T(8,128)}, u32[]{:S(2)}) copy-start(f32[256,256]{1,0:T(8,128)} %param.5) | copy-start | bytes 786436
  123.6 4.3 %collective-permute-start = (f32[8,128]{1,0:T(8,128)S(1)}, f32[8,128]{1,0:T(8,128)S(1)}, u32[]{:S(2)}, u32[]{:S(2)}) collective-permute-start(f32[8,128]{1,0:T(8,128)S(1)} %slice_reduce_fusion), channel_id=1, source_target_pairs={{0,16},{16,0},{1,17},{17,1},{2,18},{18,2},{3,19},{19,3},{4,20},{20... | collective-permute-start | bytes 12296 | tf_op jit(solution)/shard_map/ppermute | solution.py:408
  125.8 2.3 %copy-start.1 = (f32[16,32,128]{2,1,0:T(8,128)S(1)}, f32[16,32,128]{2,1,0:T(8,128)}, u32[]{:S(2)}) copy-start(f32[16,32,128]{2,1,0:T(8,128)} %get-tuple-element.14) | copy-start | bytes 786436
  128.0 0.9 copy-start.4
where the time goes:
time: 129 us
  Pallas kernels  117 us (91%)
  local copies, waits for them, and re-layouts  6.41 us (5%)
  other arithmetic  4.41 us (3%)
    pallas_call x1, Pallas kernels, local(): pl.pallas_call(functools.partial(return_kernel, n), out_shape=(jax.ShapeD...  47.5 us
    pallas_call x1, Pallas kernels, local(): pl.pallas_call(functools.partial(outward_kernel, (n, half, lp)), out_shap...  45.1 us
    pallas_call x1, Pallas kernels, local(): pl.pallas_call(functools.partial(column_kernel, (n, win, lp, nx), fill, l...  21.3 us
    pallas_call x1, Pallas kernels, local(): pl.pallas_call(functools.partial(edge_kernel, (half, lp, nx)), out_shape=...  2.64 us
  transfers between devices with their start and end apart: 1, of which 0 were waited for; matrix products, arithmetic and copies ran while one was open for 3% of the time, Pallas kernels for 0%

commit v1 on v0

v1 whole, which is shorter than its diff:
```python
import functools

import jax
import jax.numpy as jnp
from jax import lax
from jax.experimental import pallas as pl
from jax.experimental.pallas import tpu as pltpu
from jax.sharding import PartitionSpec as P

NBIN = 64
MESH = pl.DeviceIdType.MESH
PAIRS = ((0, 0), (1, 1), (2, 2), (0, 1), (0, 2), (1, 2))


def tensor_norm(s):
    diag = s[0] * s[0] + s[1] * s[1] + s[2] * s[2]
    off = s[3] * s[3] + s[4] * s[4] + s[5] * s[5]
    return jnp.sqrt(2.0 * diag + 4.0 * off)


def strain_of(dx, dy, dz):
    return [
        dx[0] * 0.5,
        dy[1] * 0.5,
        dz[2] * 0.5,
        0.25 * (dy[0] + dx[1]),
        0.25 * (dz[0] + dx[2]),
        0.25 * (dz[1] + dy[2]),
    ]


def fill_from_blocks(dims, ext, own, right, left):
    n, win, lp, nx = dims
    lane = lax.broadcasted_iota(jnp.int32, (lp, nx), 1)
    from_right = lane < nx // 2

    @pl.loop(0, n)
    def _(p):
        rows = pl.ds(pl.multiple_of(8 + p * lp, 8), lp)
        for c in range(3):
            for z in range(win):
                ext[c, z, rows, 0:nx] = own[p, c, z]
                ext[c, z, rows, nx : 2 * nx] = jnp.where(from_right, right[p, c, z], left[p, c, z])


def column_kernel(dims, fill, sources, *refs):
    n, win, lp, nx = dims
    blocks, refs = refs[:sources], refs[sources:]
    weights, onehot, back, ext, bhi, blo, filt, lms, mms, whi, wlo = refs
    zs = win - 4
    ny = n * lp
    lanes = 2 * nx
    heavy = weights[...].astype(jnp.bfloat16)
    whi[...] = heavy
    wlo[...] = (weights[...] - heavy.astype(jnp.float32)).astype(jnp.bfloat16)

    zero = jnp.zeros((8, lanes), jnp.float32)
    for c in range(3):
        for z in range(win):
            ext[c, z, 0:8, :] = zero
            ext[c, z, ny + 8 : ny + 16, :] = zero
    fill(dims, ext, *blocks)

    @pl.loop(0, n)
    def _(p):
        base = pl.multiple_of(p * lp, 8)
        u = [[ext[c, z, pl.ds(base + 8, lp), :] for z in range(win)] for c in range(3)]
        boxes = [[None] * 21 for _ in range(zs)]
        for z in range(1, win - 1):
            v = [u[c][z] for c in range(3)]
            dx, dy, dz = [], [], []
            for c in range(3):
                dx.append(pltpu.roll(v[c], lanes - 1, 1) - pltpu.roll(v[c], 1, 1))
                tall = ext[c, z, pl.ds(base, lp + 16), :]
                dy.append(tall[9 : 9 + lp] - tall[7 : 7 + lp])
                dz.append(u[c][z + 1] - u[c][z - 1])
            s = strain_of(dx, dy, dz)
            mag = tensor_norm(s)
            fields = v + s + [v[i] * v[j] for i, j in PAIRS] + [mag * t for t in s]
            for o in range(zs):
                step = z - (o + 2)
                if -1 <= step <= 1:
                    for k in range(21):
                        term = fields[k] if step else 2.0 * fields[k]
                        boxes[o][k] = term if boxes[o][k] is None else boxes[o][k] + term
        for o in range(zs):
            for k in range(21):
                f = boxes[o][k]
                box = (pltpu.roll(f, 1, 1) + pltpu.roll(f, lanes - 1, 1) + 2.0 * f)[:, :nx] * 0.0625
                high = box.astype(jnp.bfloat16)
                cols = slice(o * nx, (o + 1) * nx)
                bhi[k, pl.ds(base, lp), cols] = high
                blo[k, pl.ds(base, lp), cols] = (box - high.astype(jnp.float32)).astype(jnp.bfloat16)

    @pl.loop(0, 21)
    def _(k):
        dot = functools.partial(jnp.dot, preferred_element_type=jnp.float32)
        filt[k] = dot(whi[...], bhi[k]) + (dot(whi[...], blo[k]) + dot(wlo[...], bhi[k]))

    @pl.loop(0, n)
    def _(p):
        base = pl.multiple_of(p * lp, 8)
        lm_total = jnp.zeros((lp, nx), jnp.float32)
        mm_total = jnp.zeros((lp, nx), jnp.float32)
        for o in range(zs):
            g = [filt[k, pl.ds(base, lp), o * nx : (o + 1) * nx] for k in range(21)]
            fmag = 4.0 * tensor_norm(g[3:9])
            for q, (i, j) in enumerate(PAIRS):
                leonard = g[9 + q] - g[i] * g[j]
                model = g[15 + q] - fmag * g[3 + q]
                weighted = model if q < 3 else 2.0 * model
                lm_total += leonard * weighted
                mm_total += model * weighted
                back[p, (q * zs + o) * lp : (q * zs + o + 1) * lp, :] = leonard
        lms[pl.ds(base, lp), :] = lm_total
        mms[pl.ds(base, lp), :] = mm_total

    ones = jnp.ones((8, nx), jnp.float32)
    exact = functools.partial(
        lax.dot_general, preferred_element_type=jnp.float32, precision=lax.Precision.HIGHEST
    )
    totals = []
    for part in (lms, mms):
        planes = exact(ones, part[...], (((1,), (1,)), ((), ())))
        totals.append(exact(planes, onehot[...], (((1,), (0,)), ((), ()))))
    row = lax.broadcasted_iota(jnp.int32, (8, onehot.shape[1]), 0)
    tile = jnp.where(row < 4, totals[0], totals[1])
    for p in range(n):
        back[p, 6 * zs * lp :, :] = tile


def greet_all(m, n):
    me = lax.axis_index("px") * n + lax.axis_index("pz")
    barrier = pltpu.get_barrier_semaphore()

    @pl.loop(1, m * n)
    def _(step):
        peer = lax.rem(me + step, m * n)
        pl.semaphore_signal(barrier, inc=1, device_id=(peer // n, lax.rem(peer, n)), device_id_type=MESH)

    pl.semaphore_wait(barrier, m * n - 1)


def magnitude_kernel(centre, right, left, below, above, out):
    _, lp, nz, nx = centre.shape
    lane = lax.broadcasted_iota(jnp.int32, (nz, nx), 1)
    for y in range(lp):
        v = [centre[c, y] for c in range(3)]
        dx, dy, dz = [], [], []
        for c in range(3):
            ahead = jnp.where(lane == nx - 1, pltpu.roll(right[c, y], nx - 1, 1), pltpu.roll(v[c], nx - 1, 1))
            behind = jnp.where(lane == 0, pltpu.roll(left[c, y], 1, 1), pltpu.roll(v[c], 1, 1))
            dx.append(ahead - behind)
            dz.append(pltpu.roll(v[c], nz - 1, 0) - pltpu.roll(v[c], 1, 0))
            up = centre[c, y + 1] if y + 1 < lp else above[c, 0]
            down = centre[c, y - 1] if y else below[c, 0]
            dy.append(up - down)
        out[y] = tensor_norm(strain_of(dx, dy, dz))


def swap_bit(first, second, bit):
    nx = first.shape[-1]
    low = (lax.broadcasted_iota(jnp.int32, first.shape, 1) & bit) == 0
    return (
        jnp.where(low, first, pltpu.roll(second, bit, 1)),
        jnp.where(low, pltpu.roll(first, nx - bit, 1), second),
    )


def pack_kernel(dims, velocity, packed):
    lp, nz, nx = dims
    groups = nx // nz
    steps = lp // groups

    @pl.loop(0, 3)
    def _(c):
        for q in range(steps):
            rows = jnp.concatenate([velocity[c, g * steps + q] for g in range(groups)], axis=0)
            packed[c, pl.ds(q, nx, stride=steps), :] = rows.T


def spread_kernel(dims, packed, held, main_out, left_out, right_out, pass_out, main_in, edge_in, pass_in):
    n, h, pairs = dims
    a, s = lax.axis_index("px"), lax.axis_index("pz")
    greet_all(2, n)

    def send(source, dst, core, chip, out_sem, in_sem):
        itself = (core == a) & (chip == s)
        copy = pltpu.make_async_remote_copy(
            source, dst, out_sem, in_sem, device_id=(core, chip), device_id_type=MESH
        )
        return itself, copy, pltpu.make_async_copy(source, dst, in_sem)

    def sends(i):
        chip = h * a + i
        whole = 2 * pairs
        for core in range(2):
            source = packed.at[:, pl.ds(whole * i + pairs * core, pairs)]
            yield send(source, held.at[s, :, 1 : pairs + 1], core, chip, main_out.at[i, core], main_in.at[s])
        source = packed.at[:, pl.ds(whole * i + whole - 1, 1)]
        yield send(source, held.at[s, :, 0:1], 0, lax.rem(chip + 1, n), left_out.at[i], edge_in.at[s])
        source = packed.at[:, pl.ds(whole * i, 1)]
        yield send(source, held.at[s, :, pairs + 1 : pairs + 2], 1, lax.rem(chip + n - 1, n), right_out.at[i], edge_in.at[s])

    @pl.loop(0, h)
    def _(r):
        for itself, copy, here in sends(lax.rem(s + r, h)):
            pl.when(itself)(here.start)
            pl.when(jnp.logical_not(itself))(copy.start)

    def forward(p):
        source = held.at[p, :, pl.ds(pairs - (pairs - 1) * a, 1)]
        return pltpu.make_async_remote_copy(
            source, held.at[p, :, pl.ds((pairs + 1) * a, 1)], pass_out.at[p], pass_in.at[p],
            device_id=(1 - a, s), device_id_type=MESH,
        )

    @pl.loop(0, n)
    def _(i):
        p = lax.rem(s + n - i, n)
        pltpu.make_async_copy(packed.at[:, 0:pairs], held.at[p, :, 1 : pairs + 1], main_in.at[p]).wait()
        forward(p).start()

    @pl.loop(0, n)
    def _(p):
        forward(p).wait()
        pltpu.make_async_copy(packed.at[:, 0:1], held.at[p, :, 0:1], edge_in.at[p]).wait()

    @pl.loop(0, h)
    def _(i):
        for itself, copy, here in sends(i):
            pl.when(jnp.logical_not(itself))(copy.wait_send)


def plane_order(shape, lp, nx, dim):
    at = lax.broadcasted_iota(jnp.int32, shape, dim)
    return (at % nx) // 8 * lp + at // nx * 8 + at % 8


def column_weights(dims, inverse, block, bins, whi, wlo, onehot):
    ny, lp, nx = dims
    label = jnp.broadcast_to(block[...].astype(jnp.float32), (ny, ny))
    masked = jnp.where(label == label.T, inverse[...], 0.0)
    weights = masked / jnp.sum(masked, axis=1, keepdims=True) * 0.0625
    order = plane_order((ny, ny), lp, nx, 0) == lax.broadcasted_iota(jnp.int32, (ny, ny), 1)
    order = order.astype(jnp.float32).astype(jnp.bfloat16)
    across = functools.partial(
        lax.dot_general, dimension_numbers=(((1,), (1,)), ((), ())), preferred_element_type=jnp.float32
    )

    def placed(part):
        turned = across(order, part).astype(jnp.bfloat16)
        return across(turned, order).astype(jnp.bfloat16)

    heavy = weights.astype(jnp.bfloat16)
    whi[...] = placed(heavy)
    wlo[...] = placed((weights - heavy.astype(jnp.float32)).astype(jnp.bfloat16))
    label = jnp.broadcast_to(bins[...], (nx, ny))
    hot = (label == lax.broadcasted_iota(jnp.int32, (nx, ny), 0)).astype(jnp.float32)
    onehot[...] = across(hot.astype(jnp.bfloat16), order)


def strip_kernel(dims, held, inverse, block, bins, back, u, fields, filt, stress, whi, wlo, onehot, sums):
    n, pairs, lp, nz, nx = dims
    ny, groups = n * lp, nx // nz
    halves = lp // 8
    across = 2 * pairs
    tiles = nz // 8
    column_weights((ny, lp, nx), inverse, block, bins, whi, wlo, onehot)

    @pl.loop(0, 3)
    def _(c):
        for p in range(pairs + 2):
            turned = held[:, c, p].reshape(nx, nx).T
            for hf in range(halves):
                first = turned[2 * hf * nz : (2 * hf + 1) * nz]
                second = turned[(2 * hf + 1) * nz : (2 * hf + 2) * nz]
                u[c, hf, 2 * p], u[c, hf, 2 * p + 1] = swap_bit(first, second, 4)

    lane = lax.broadcasted_iota(jnp.int32, (nz, nx), 1)
    last, first_lane = lane % 8 == 7, lane % 8 == 0
    top, bottom = lane == nx - 1, lane == 0

    @pl.loop(0, across + 2)
    def _(x):
        here, dx, dy, dz = [], [], [], []
        for c in range(3):
            v = [u[c, hf, x + 1] for hf in range(2)]
            here.append(v)
            dx.append([u[c, hf, x + 2] - u[c, hf, x] for hf in range(2)])
            dz.append([pltpu.roll(v[hf], nz - 1, 0) - pltpu.roll(v[hf], 1, 0) for hf in range(2)])
            ahead = [pltpu.roll(v[hf], nx - 1, 1) for hf in range(2)]
            behind = [pltpu.roll(v[hf], 1, 1) for hf in range(2)]
            up = [
                jnp.where(last, pltpu.roll(v[1], 7, 1), ahead[0]),
                jnp.where(last, jnp.where(top, 0.0, ahead[0]), ahead[1]),
            ]
            down = [
                jnp.where(first_lane, jnp.where(bottom, 0.0, behind[1]), behind[0]),
                jnp.where(first_lane, pltpu.roll(v[0], nx - 7, 1), behind[1]),
            ]
            dy.append([up[hf] - down[hf] for hf in range(2)])
        for hf in range(2):
            gx, gy, gz = [d[hf] for d in dx], [d[hf] for d in dy], [d[hf] for d in dz]
            s = [gx[0] + gx[0], gy[1] + gy[1], gz[2] + gz[2], gy[0] + gx[1], gz[0] + gx[2], gz[1] + gy[2]]
            mag = tensor_norm(s)
            for c in range(3):
                fields[c, x, hf] = here[c][hf]
            for q, (i, j) in enumerate(PAIRS):
                fields[3 + q, x, hf] = s[q]
                fields[9 + q, x, hf] = here[i][hf] * here[j][hf]
                fields[15 + q, x, hf] = mag * s[q]

    @pl.loop(0, 21)
    def _(k):
        columns = []
        for hf in range(2):
            pair = [fields[k, x, hf] + fields[k, x + 1, hf] for x in range(across + 1)]
            rows = []
            for x in range(across):
                along = pair[x] + pair[x + 1]
                rows.append(pltpu.roll(along, 1, 0) + pltpu.roll(along, nz - 1, 0) + (along + along))
            columns.append(jnp.concatenate(rows, axis=0))
        box = jnp.concatenate(columns, axis=1)
        high = box.astype(jnp.bfloat16)
        low = (box - high.astype(jnp.float32)).astype(jnp.bfloat16)
        dot = functools.partial(jnp.dot, preferred_element_type=jnp.float32)
        filt[k] = dot(high, whi[...]) + (dot(low, whi[...]) + dot(high, wlo[...]))

    sums[...] = jnp.zeros(sums.shape, jnp.float32)

    @pl.loop(0, across * tiles)
    def _(r):
        rows = pl.ds(pl.multiple_of(8 * r, 8), 8)
        for hf in range(2):
            cols = slice(hf * nx, (hf + 1) * nx)
            g = [filt[k, rows, cols] for k in range(21)]
            fmag = 4.0 * tensor_norm(g[3:9])
            lm_total = jnp.zeros((8, nx), jnp.float32)
            mm_total = jnp.zeros((8, nx), jnp.float32)
            for q, (i, j) in enumerate(PAIRS):
                leonard = g[9 + q] - g[i] * g[j]
                model = g[15 + q] - fmag * g[3 + q]
                weighted = model if q < 3 else 2.0 * model
                lm_total += leonard * weighted
                mm_total += model * weighted
                stress[q, hf, rows, :] = leonard
            sums[0, :, cols] += lm_total
            sums[1, :, cols] += mm_total

    @pl.loop(0, 6)
    def _(f):
        for p in range(pairs):
            rows = []
            for hf in range(halves):
                first = stress[f, hf, 2 * p * nz : (2 * p + 1) * nz, :]
                second = stress[f, hf, (2 * p + 1) * nz : (2 * p + 2) * nz, :]
                rows.extend(swap_bit(first, second, 4))
            turned = jnp.concatenate(rows, axis=0).T
            at = pl.ds(pl.multiple_of((f * pairs + p) * 8, 8), 8)
            back[:, at, :] = turned.reshape(n, 8, nx)

    exact = functools.partial(
        lax.dot_general, dimension_numbers=(((1,), (1,)), ((), ())),
        preferred_element_type=jnp.float32, precision=lax.Precision.HIGHEST,
    )
    lm_bins = jnp.sum(exact(sums[0], onehot[...]), axis=0, keepdims=True) * (1.0 / 16.0)
    mm_bins = jnp.sum(exact(sums[1], onehot[...]), axis=0, keepdims=True) * (1.0 / 256.0)
    row = lax.broadcasted_iota(jnp.int32, (8, nx), 0)
    tile = jnp.where(row < 4, lm_bins, mm_bins)
    for p in range(n):
        back[p, 6 * pairs * 8 :, :] = tile


def gather_kernel(n, back, velocity, home, sums, out, beside, near, back_out, back_in, sum_out, sum_in, halo_out, halo_in):
    _, lp, nz, nx = velocity.shape
    a, s = lax.axis_index("px"), lax.axis_index("pz")
    h = n // 2
    rows = back.shape[1] - 8
    greet_all(2, n)
    slot = 2 * lax.rem(s, h) + a
    half = s // h
    remote = functools.partial(pltpu.make_async_remote_copy, device_id_type=MESH)
    halos = [
        remote(velocity, beside, halo_out.at[0], halo_in.at[0], device_id=(1 - a, s)),
        remote(velocity.at[:, lp - 1], near.at[0], halo_out.at[1], halo_in.at[1], device_id=(a, lax.rem(s + 1, n))),
        remote(velocity.at[:, 0], near.at[1], halo_out.at[2], halo_in.at[2], device_id=(a, lax.rem(s + n - 1, n))),
    ]
    for copy in halos:
        copy.start()

    def send(source, dst, core, chip, out_sem, in_sem):
        itself = (core == a) & (chip == s)
        copy = remote(source, dst, out_sem, in_sem, device_id=(core, chip))
        return itself, copy, pltpu.make_async_copy(source, dst, in_sem)

    def sends(p):
        yield send(back.at[p], home.at[slot], half, p, back_out.at[p], back_in.at[slot])
        yield send(back.at[p, pl.ds(rows, 8)], sums.at[slot], 1 - half, p, sum_out.at[p], sum_in.at[slot])

    @pl.loop(0, n)
    def _(i):
        for itself, copy, here in sends(lax.rem(s + i, n)):
            pl.when(itself)(here.start)
            pl.when(jnp.logical_not(itself))(copy.start)

    for copy in halos:
        copy.wait()
    lane = lax.broadcasted_iota(jnp.int32, (nz, nx), 1)
    has_below = (s > 0).astype(jnp.float32)
    has_above = (s < n - 1).astype(jnp.float32)

    def plane(y, ups, downs):
        dx, dy, dz = [], [], []
        for c in range(3):
            v, side = velocity[c, y], beside[c, y]
            ahead = jnp.where(lane == nx - 1, pltpu.roll(side, nx - 1, 1), pltpu.roll(v, nx - 1, 1))
            behind = jnp.where(lane == 0, pltpu.roll(side, 1, 1), pltpu.roll(v, 1, 1))
            dx.append(ahead - behind)
            dz.append(pltpu.roll(v, nz - 1, 0) - pltpu.roll(v, 1, 0))
            dy.append(ups[c] - downs[c])
        out[y] = tensor_norm(strain_of(dx, dy, dz))

    line = [near[0, c] * has_below for c in range(3)]
    plane(0, [velocity[c, 1] for c in range(3)], line)
    line = [near[1, c] * has_above for c in range(3)]
    plane(lp - 1, line, [velocity[c, lp - 2] for c in range(3)])

    @pl.loop(1, lp - 1)
    def _(y):
        plane(y, [velocity[c, y + 1] for c in range(3)], [velocity[c, y - 1] for c in range(3)])

    @pl.loop(0, n)
    def _(p):
        pltpu.make_async_copy(back.at[0], home.at[p], back_in.at[p]).wait()
        pltpu.make_async_copy(back.at[0, pl.ds(rows, 8)], sums.at[p], sum_in.at[p]).wait()
        for itself, copy, here in sends(p):
            pl.when(jnp.logical_not(itself))(copy.wait_send)


def finish_kernel(dims, cells, chip, home, sums, magnitude, bins, leonard, viscosity, coefficient):
    n, pairs, lp, nz, nx = dims
    ny, groups = n * lp, nx // nz
    steps = lp // groups
    rows = 6 * pairs * 8
    total = home[0, rows:, :] + sums[0]
    for p in range(1, n):
        total = total + (home[p, rows:, :] + sums[p])
    numer, denom = total[0:1, :], total[4:5, :]
    per_bin = numer / jnp.maximum(denom, jnp.float32(cells))
    exact = functools.partial(
        lax.dot_general, preferred_element_type=jnp.float32, precision=lax.Precision.HIGHEST
    )
    label = jnp.broadcast_to(bins[...].astype(jnp.float32), (nx, ny))
    kind = lax.broadcasted_iota(jnp.int32, (nx, ny), 0).astype(jnp.float32)
    onehot = (label == kind).astype(jnp.float32)
    table = jnp.broadcast_to(per_bin, (nx, nx))
    coefficient[...] = exact(table[0:8], onehot, (((1,), (0,)), ((), ())))[0:1, :]
    mine = jnp.zeros((nx, lp), jnp.float32)
    for s in range(n):
        mine = jnp.where(chip[0] == s, onehot[:, s * lp : (s + 1) * lp], mine)
    spread = exact(mine, table, (((0,), (1,)), ((), ())))
    for y in range(lp):
        viscosity[y] = spread[y : y + 1, :] * magnitude[y]

    @pl.loop(0, 6)
    def _(f):
        for q in range(steps):
            at = pl.ds(f * pairs * 8 + q, nx // n, stride=steps)
            turned = jnp.concatenate([home[p, at, :] for p in range(n)], axis=0).T
            for g in range(groups):
                leonard[f, g * steps + q] = turned[g * nz : (g + 1) * nz]


def by_strips(velocity, filter_inverse, filter_block, plane_bin, n):
    _, lp, nz, nx = velocity.shape
    ny, h = n * lp, n // 2
    pairs = nx // h // 4
    dims = (n, pairs, lp, nz, nx)
    steps = lp // (nx // nz)
    chip = lax.axis_index("pz").astype(jnp.int32).reshape(1)
    block = filter_block.reshape(1, ny)
    bins = plane_bin.reshape(1, ny)
    vmem = pl.BlockSpec(memory_space=pltpu.VMEM)
    smem = pl.BlockSpec(memory_space=pltpu.SMEM)
    f32 = functools.partial(jax.ShapeDtypeStruct, dtype=jnp.float32)
    dma = pltpu.SemaphoreType.DMA
    cells = 2 * pairs * nz

    packed = pl.pallas_call(
        functools.partial(pack_kernel, (lp, nz, nx)),
        out_shape=f32((3, nx * steps, nx)),
        in_specs=[vmem],
        out_specs=vmem,
    )(velocity)
    held = pl.pallas_call(
        functools.partial(spread_kernel, (n, h, pairs)),
        out_shape=f32((n, 3, pairs + 2, 8, nx)),
        in_specs=[vmem],
        out_specs=vmem,
        scratch_shapes=[dma((h, 2)), dma((h,)), dma((h,)), dma((n,)), dma((n,)), dma((n,)), dma((n,))],
        compiler_params=pltpu.CompilerParams(collective_id=0, has_side_effects=True),
    )(packed.reshape(3, nx * steps // 8, 8, nx))
    back = pl.pallas_call(
        functools.partial(strip_kernel, dims),
        out_shape=f32((n, 6 * pairs * 8 + 8, nx)),
        in_specs=[vmem] * 4,
        out_specs=vmem,
        scratch_shapes=[
            pltpu.VMEM((3, 2, 2 * pairs + 4, nz, nx), jnp.float32),
            pltpu.VMEM((21, 2 * pairs + 2, 2, nz, nx), jnp.float32),
            pltpu.VMEM((21, cells, ny), jnp.float32),
            pltpu.VMEM((6, 2, cells, nx), jnp.float32),
            pltpu.VMEM((ny, ny), jnp.bfloat16),
            pltpu.VMEM((ny, ny), jnp.bfloat16),
            pltpu.VMEM((nx, ny), jnp.float32),
            pltpu.VMEM((2, 8, ny), jnp.float32),
        ],
        compiler_params=pltpu.CompilerParams(vmem_limit_bytes=60 * 1024 * 1024),
    )(held, filter_inverse, block, bins)
    home, sums, magnitude = pl.pallas_call(
        functools.partial(gather_kernel, n),
        out_shape=(f32(back.shape), f32((n, 8, nx)), f32((lp, nz, nx))),
        in_specs=[vmem] * 2,
        out_specs=(vmem,) * 3,
        scratch_shapes=[
            pltpu.VMEM((3, lp, nz, nx), jnp.float32),
            pltpu.VMEM((2, 3, nz, nx), jnp.float32),
            dma((n,)),
            dma((n,)),
            dma((n,)),
            dma((n,)),
            dma((3,)),
            dma((3,)),
        ],
        compiler_params=pltpu.CompilerParams(collective_id=1, has_side_effects=True),
    )(back, velocity)
    leonard, viscosity, coefficient = pl.pallas_call(
        functools.partial(finish_kernel, dims, 2 * nx * nz),
        out_shape=(f32((6, lp, nz, nx)), f32((lp, nz, nx)), f32((1, ny))),
        in_specs=[smem] + [vmem] * 4,
        out_specs=(vmem,) * 3,
    )(chip, home, sums, magnitude, bins)
    return (leonard, viscosity, coefficient.reshape(ny))


def by_blocks(velocity, filter_inverse, filter_block, plane_bin):
    _, lp, nz, nx = velocity.shape
    n = lax.axis_size("pz")
    m = lax.axis_size("px")
    ny, zs = n * lp, nz // n
    win = zs + 4

    same = (filter_block[:, None] == filter_block[None, :]).astype(jnp.float32)
    masked = filter_inverse * same
    weights = masked / jnp.sum(masked, axis=1, keepdims=True)
    onehot = (plane_bin[:, None] == jnp.arange(nx, dtype=jnp.int32)[None, :]).astype(jnp.float32)

    right = lax.ppermute(velocity, "px", [((i + 1) % m, i) for i in range(m)])
    left = right if m == 2 else lax.ppermute(velocity, "px", [(i, (i + 1) % m) for i in range(m)])
    below = lax.ppermute(velocity[:, -1:], "pz", [(i, i + 1) for i in range(n - 1)])
    above = lax.ppermute(velocity[:, :1], "pz", [(i + 1, i) for i in range(n - 1)])
    magnitude = pl.pallas_call(
        magnitude_kernel,
        out_shape=jax.ShapeDtypeStruct((lp, nz, nx), jnp.float32),
        cost_estimate=pl.CostEstimate(flops=60 * lp * nz * nx, bytes_accessed=40 * lp * nz * nx, transcendentals=0),
    )(velocity, right, left, below, above)
    turned = jnp.transpose(velocity, (0, 2, 1, 3))
    turned = jnp.concatenate([turned[:, -2:], turned, turned[:, :2]], axis=1)
    sent = jnp.stack([turned[:, t * zs : t * zs + win] for t in range(n)])
    own = lax.all_to_all(sent, "pz", split_axis=0, concat_axis=0, tiled=True)
    ahead = lax.ppermute(own, "px", [((i + 1) % m, i) for i in range(m)])
    behind = lax.ppermute(own, "px", [(i, (i + 1) % m) for i in range(m)])
    blocks = (own, ahead, behind)

    rows = 6 * zs * lp
    back = pl.pallas_call(
        functools.partial(column_kernel, (n, win, lp, nx), fill_from_blocks, len(blocks)),
        out_shape=jax.ShapeDtypeStruct((n, rows + 8, nx), jnp.float32),
        in_specs=[pl.BlockSpec(memory_space=pltpu.VMEM)] * 5,
        out_specs=pl.BlockSpec(memory_space=pltpu.VMEM),
        scratch_shapes=[
            pltpu.VMEM((3, win, ny + 16, 2 * nx), jnp.float32),
            pltpu.VMEM((21, ny, zs * nx), jnp.bfloat16),
            pltpu.VMEM((21, ny, zs * nx), jnp.bfloat16),
            pltpu.VMEM((21, ny, zs * nx), jnp.float32),
            pltpu.VMEM((ny, nx), jnp.float32),
            pltpu.VMEM((ny, nx), jnp.float32),
            pltpu.VMEM((ny, ny), jnp.bfloat16),
            pltpu.VMEM((ny, ny), jnp.bfloat16),
        ],
        compiler_params=pltpu.CompilerParams(vmem_limit_bytes=60 * 1024 * 1024),
    )(*blocks, weights, onehot)

    home = lax.all_to_all(back, "pz", split_axis=0, concat_axis=0, tiled=True)
    totals = lax.psum(jnp.sum(home[:, rows:], axis=0), "px")
    stress = home[:, :rows].reshape(n, 6, zs, lp, nx)
    leonard = jnp.transpose(stress, (1, 3, 0, 2, 4)).reshape(6, lp, nz, nx)
    numer, denom = totals[0, :NBIN], totals[4, :NBIN]
    cells = nx * m * nz
    per_bin = numer / jnp.maximum(denom, jnp.float32(cells))
    coefficient = jnp.dot(onehot[:, :NBIN], per_bin, precision=lax.Precision.HIGHEST)
    local_coef = lax.dynamic_slice_in_dim(coefficient, lax.axis_index("pz") * lp, lp, 0)
    viscosity = local_coef[:, None, None] * magnitude
    return (leonard, viscosity, coefficient)


def local(*arrays):
    _, lp, nz, nx = arrays[0].shape
    n, m = lax.axis_size("pz"), lax.axis_size("px")
    groups = nx // nz
    fits = m == 2 and n % 2 == 0 and 8 * n == nx and groups * nz == nx and lp == 16 and groups == 4
    if fits:
        return by_strips(*arrays, n)
    return by_blocks(*arrays)


def solution(mesh):
    return jax.shard_map(
        local,
        mesh=mesh,
        in_specs=(P(None, "pz", None, "px"), P(), P(), P()),
        out_specs=(P(None, "pz", None, "px"), P("pz", None, "px"), P()),
        check_vma=False,
    )
```

time: 129 us -> 105 us (0.81)
  the two profiles are of different devices: /device:TPU:31 before, /device:TPU:15 now
where the time goes in v1:
time: 105 us; the launch traced here: 104 us
  Pallas kernels  104 us (99%)
    pallas_call x1, Pallas kernels, by_strips(): pl.pallas_call(functools.partial(gather_kernel, n), out_shape=(f32(back.s...  50.7 us
    pallas_call x1, Pallas kernels, by_strips(): pl.pallas_call(functools.partial(spread_kernel, (n, h, pairs)), out_shape...  31.2 us
    pallas_call x1, Pallas kernels, by_strips(): pl.pallas_call(functools.partial(strip_kernel, dims), out_shape=f32((n, 6...  14.6 us
    pallas_call x1, Pallas kernels, by_strips(): pl.pallas_call(functools.partial(finish_kernel, dims, 2 * nx * nz), out_s...  4.86 us
    pallas_call x1, Pallas kernels, by_strips(): pl.pallas_call(functools.partial(pack_kernel, (lp, nz, nx)), out_shape=f3...  2.42 us

profile of v1, /device:TPU:15, one launch (start us, length us, event | category | flops | bytes accessed | tf_op | source)
XLA Modules:
  0.0 104.4 jit_solution(12078666814477137224)
XLA Ops:
  0.6 2.4 %shard_map.67 = f32[3,512,128]{2,1,0:T(8,128)} custom-call(f32[3,16,32,128]{3,2,1,0:T(8,128)} %velocity.3), custom_call_target="tpu_custom_call" | custom-call | tf_op jit(solution)/shard_map/pallas_call | solution.py:490
  3.1 31.2 %shard_map.68.held = f32[16,3,6,8,128]{4,3,2,1,0:T(8,128)} custom-call(f32[3,64,8,128]{3,2,1,0:T(8,128)} %bitcast.5), custom_call_target="tpu_custom_call" | custom-call | tf_op jit(solution)/shard_map/pallas_call | solution.py:496
  34.3 14.6 %shard_map.69.back = f32[16,200,128]{2,1,0:T(8,128)} custom-call(f32[16,3,6,8,128]{4,3,2,1,0:T(8,128)} %shard_map.68.held, f32[256,256]{1,0:T(8,128)} %inverse.1, s32[1,256]{1,0:T(1,128)} %bitcast.8, s32[1,256]{1,0:T(1,128)} %bitcast.6), custom_call_target="tpu_custom_call" | custom-call | tf_op jit(solution)/shard_map/pallas_call | solution.py:504
  48.8 50.7 %shard_map.70 = (f32[16,200,128]{2,1,0:T(8,128)}, f32[16,8,128]{2,1,0:T(8,128)}, f32[16,32,128]{2,1,0:T(8,128)}) custom-call(f32[16,200,128]{2,1,0:T(8,128)} %shard_map.69.back, f32[3,16,32,128]{3,2,1,0:T(8,128)} %velocity.3), custom_call_target="tpu_custom_call" | custom-call | tf_op jit(solution)/shard_map/pallas_call | solution.py:521
  99.6 4.9 %shard_map.71 = (f32[6,16,32,128]{3,2,1,0:T(8,128)}, f32[16,32,128]{2,1,0:T(8,128)}, f32[1,256]{1,0:T(1,128)}) custom-call(s32[1]{0:T(128)} %bitcast.chip, f32[16,200,128]{2,1,0:T(8,128)} %get-tuple-element.9.home, f32[16,8,128]{2,1,0:T(8,128)} %get-tuple-element.10.sums, f32[16,32,128]{2,1,0:T(8,128)} %get-tuple-element.11.magnitude, s32[1,256]{1,0:T(1,128)} %bitcast.7), custom_call_target="tpu_custom_call" | custom-call | tf_op jit(solution)/shard_map/pallas_call | solution.py:538

commit v2 on v1

--- a/solution.py
+++ b/solution.py
@@ -179,59 +179,6 @@
             packed[c, pl.ds(q, nx, stride=steps), :] = rows.T
 
 
-def spread_kernel(dims, packed, held, main_out, left_out, right_out, pass_out, main_in, edge_in, pass_in):
-    n, h, pairs = dims
-    a, s = lax.axis_index("px"), lax.axis_index("pz")
-    greet_all(2, n)
-
-    def send(source, dst, core, chip, out_sem, in_sem):
-        itself = (core == a) & (chip == s)
-        copy = pltpu.make_async_remote_copy(
-            source, dst, out_sem, in_sem, device_id=(core, chip), device_id_type=MESH
-        )
-        return itself, copy, pltpu.make_async_copy(source, dst, in_sem)
-
-    def sends(i):
-        chip = h * a + i
-        whole = 2 * pairs
-        for core in range(2):
-            source = packed.at[:, pl.ds(whole * i + pairs * core, pairs)]
-            yield send(source, held.at[s, :, 1 : pairs + 1], core, chip, main_out.at[i, core], main_in.at[s])
-        source = packed.at[:, pl.ds(whole * i + whole - 1, 1)]
-        yield send(source, held.at[s, :, 0:1], 0, lax.rem(chip + 1, n), left_out.at[i], edge_in.at[s])
-        source = packed.at[:, pl.ds(whole * i, 1)]
-        yield send(source, held.at[s, :, pairs + 1 : pairs + 2], 1, lax.rem(chip + n - 1, n), right_out.at[i], edge_in.at[s])
-
-    @pl.loop(0, h)
-    def _(r):
-        for itself, copy, here in sends(lax.rem(s + r, h)):
-            pl.when(itself)(here.start)
-            pl.when(jnp.logical_not(itself))(copy.start)
-
-    def forward(p):
-        source = held.at[p, :, pl.ds(pairs - (pairs - 1) * a, 1)]
-        return pltpu.make_async_remote_copy(
-            source, held.at[p, :, pl.ds((pairs + 1) * a, 1)], pass_out.at[p], pass_in.at[p],
-            device_id=(1 - a, s), device_id_type=MESH,
-        )
-
-    @pl.loop(0, n)
-    def _(i):
-        p = lax.rem(s + n - i, n)
-        pltpu.make_async_copy(packed.at[:, 0:pairs], held.at[p, :, 1 : pairs + 1], main_in.at[p]).wait()
-        forward(p).start()
-
-    @pl.loop(0, n)
-    def _(p):
-        forward(p).wait()
-        pltpu.make_async_copy(packed.at[:, 0:1], held.at[p, :, 0:1], edge_in.at[p]).wait()
-
-    @pl.loop(0, h)
-    def _(i):
-        for itself, copy, here in sends(i):
-            pl.when(jnp.logical_not(itself))(copy.wait_send)
-
-
 def plane_order(shape, lp, nx, dim):
     at = lax.broadcasted_iota(jnp.int32, shape, dim)
     return (at % nx) // 8 * lp + at // nx * 8 + at % 8
@@ -260,34 +207,62 @@
     onehot[...] = across(hot.astype(jnp.bfloat16), order)
 
 
-def strip_kernel(dims, held, inverse, block, bins, back, u, fields, filt, stress, whi, wlo, onehot, sums):
-    n, pairs, lp, nz, nx = dims
-    ny, groups = n * lp, nx // nz
-    halves = lp // 8
-    across = 2 * pairs
-    tiles = nz // 8
-    column_weights((ny, lp, nx), inverse, block, bins, whi, wlo, onehot)
-
+def flip_bits(value, mask, count):
+    out = 0
+    for bit in range(count):
+        digit = lax.rem(value // (1 << bit), 2)
+        out = out + (1 << bit) * ((1 - digit) if mask >> bit & 1 else digit)
+    return out
+
+
+def plane_magnitudes(velocity, beside, near, out, has_below, has_above):
+    _, lp, nz, nx = velocity.shape
+    lane = lax.broadcasted_iota(jnp.int32, (nz, nx), 1)
+
+    def plane(y, ups, downs):
+        dx, dy, dz = [], [], []
+        for c in range(3):
+            v, side = velocity[c, y], beside[c, y]
+            ahead = jnp.where(lane == nx - 1, pltpu.roll(side, nx - 1, 1), pltpu.roll(v, nx - 1, 1))
+            behind = jnp.where(lane == 0, pltpu.roll(side, 1, 1), pltpu.roll(v, 1, 1))
+            dx.append(ahead - behind)
+            dz.append(pltpu.roll(v, nz - 1, 0) - pltpu.roll(v, 1, 0))
+            dy.append(ups[c] - downs[c])
+        out[y] = tensor_norm(strain_of(dx, dy, dz))
+
+    line = [near[0, c] * has_below for c in range(3)]
+    plane(0, [velocity[c, 1] for c in range(3)], line)
+    line = [near[1, c] * has_above for c in range(3)]
+    plane(lp - 1, line, [velocity[c, lp - 2] for c in range(3)])
+
+    @pl.loop(1, lp - 1)
+    def _(y):
+        plane(y, [velocity[c, y + 1] for c in range(3)], [velocity[c, y - 1] for c in range(3)])
+
+
+def unpack_pair(held, u, slot, nz, nx):
     @pl.loop(0, 3)
     def _(c):
-        for p in range(pairs + 2):
-            turned = held[:, c, p].reshape(nx, nx).T
-            for hf in range(halves):
-                first = turned[2 * hf * nz : (2 * hf + 1) * nz]
-                second = turned[(2 * hf + 1) * nz : (2 * hf + 2) * nz]
-                u[c, hf, 2 * p], u[c, hf, 2 * p + 1] = swap_bit(first, second, 4)
-
+        turned = held[:, c, slot].reshape(nx, nx).T
+        for hf in range(2):
+            first = turned[2 * hf * nz : (2 * hf + 1) * nz]
+            second = turned[(2 * hf + 1) * nz : (2 * hf + 2) * nz]
+            u[c, hf, 2 * slot], u[c, hf, 2 * slot + 1] = swap_bit(first, second, 4)
+
+
+def field_columns(u, fields, start, count, nz, nx):
     lane = lax.broadcasted_iota(jnp.int32, (nz, nx), 1)
     last, first_lane = lane % 8 == 7, lane % 8 == 0
     top, bottom = lane == nx - 1, lane == 0
 
-    @pl.loop(0, across + 2)
-    def _(x):
+    @pl.loop(0, count)
+    def _(i):
+        x = start + i
         here, dx, dy, dz = [], [], [], []
         for c in range(3):
-            v = [u[c, hf, x + 1] for hf in range(2)]
+            v = [u[c, hf, x] for hf in range(2)]
             here.append(v)
-            dx.append([u[c, hf, x + 2] - u[c, hf, x] for hf in range(2)])
+            dx.append([u[c, hf, x + 1] - u[c, hf, x - 1] for hf in range(2)])
             dz.append([pltpu.roll(v[hf], nz - 1, 0) - pltpu.roll(v[hf], 1, 0) for hf in range(2)])
             ahead = [pltpu.roll(v[hf], nx - 1, 1) for hf in range(2)]
             behind = [pltpu.roll(v[hf], 1, 1) for hf in range(2)]
@@ -311,30 +286,44 @@
                 fields[9 + q, x, hf] = here[i][hf] * here[j][hf]
                 fields[15 + q, x, hf] = mag * s[q]
 
+
+def filter_pair(fields, start, high, low, filt, whi, wlo, nz):
+    cells = 2 * nz
+
     @pl.loop(0, 21)
     def _(k):
         columns = []
         for hf in range(2):
-            pair = [fields[k, x, hf] + fields[k, x + 1, hf] for x in range(across + 1)]
+            f = [fields[k, start + i, hf] for i in range(4)]
+            pair = [f[i] + f[i + 1] for i in range(3)]
             rows = []
-            for x in range(across):
-                along = pair[x] + pair[x + 1]
+            for i in range(2):
+                along = pair[i] + pair[i + 1]
                 rows.append(pltpu.roll(along, 1, 0) + pltpu.roll(along, nz - 1, 0) + (along + along))
             columns.append(jnp.concatenate(rows, axis=0))
         box = jnp.concatenate(columns, axis=1)
-        high = box.astype(jnp.bfloat16)
-        low = (box - high.astype(jnp.float32)).astype(jnp.bfloat16)
+        heavy = box.astype(jnp.bfloat16)
+        at = pl.ds(pl.multiple_of(k * cells, cells), cells)
+        high[at, :] = heavy
+        low[at, :] = (box - heavy.astype(jnp.float32)).astype(jnp.bfloat16)
+
+    @pl.loop(0, 3)
+    def _(b):
         dot = functools.partial(jnp.dot, preferred_element_type=jnp.float32)
-        filt[k] = dot(high, whi[...]) + (dot(low, whi[...]) + dot(high, wlo[...]))
-
-    sums[...] = jnp.zeros(sums.shape, jnp.float32)
-
-    @pl.loop(0, across * tiles)
+        at = pl.ds(pl.multiple_of(b * 7 * cells, cells), 7 * cells)
+        head, rest = high[at, :], low[at, :]
+        filt[at, :] = dot(head, whi[...]) + (dot(rest, whi[...]) + dot(head, wlo[...]))
+
+
+def stress_pair(filt, stress, sums, nz, nx):
+    cells = 2 * nz
+
+    @pl.loop(0, cells // 8)
     def _(r):
-        rows = pl.ds(pl.multiple_of(8 * r, 8), 8)
+        base = pl.multiple_of(8 * r, 8)
         for hf in range(2):
             cols = slice(hf * nx, (hf + 1) * nx)
-            g = [filt[k, rows, cols] for k in range(21)]
+            g = [filt[pl.ds(base + k * cells, 8), cols] for k in range(21)]
             fmag = 4.0 * tensor_norm(g[3:9])
             lm_total = jnp.zeros((8, nx), jnp.float32)
             mm_total = jnp.zeros((8, nx), jnp.float32)
@@ -344,21 +333,132 @@
                 weighted = model if q < 3 else 2.0 * model
                 lm_total += leonard * weighted
                 mm_total += model * weighted
-                stress[q, hf, rows, :] = leonard
+                stress[q, hf, pl.ds(base, 8), :] = leonard
             sums[0, :, cols] += lm_total
             sums[1, :, cols] += mm_total
 
-    @pl.loop(0, 6)
-    def _(f):
-        for p in range(pairs):
+
+def flow_kernel(
+    dims, packed, velocity, inverse, block, bins, home, totals, magnitude,
+    held, u, fields, high, low, filt, stress, back, whi, wlo, onehot, sums, tile, beside, near,
+    main_out, edge_out, pass_out, back_out, sum_out, halo_out,
+    main_in, edge_in, pass_in, back_in, sum_in, halo_in,
+):
+    n, pairs, lp, nz, nx = dims
+    ny, h = n * lp, n // 2
+    bits = n.bit_length() - 1
+    whole = 2 * pairs
+    a, s = lax.axis_index("px"), lax.axis_index("pz")
+    remote = functools.partial(pltpu.make_async_remote_copy, device_id_type=MESH)
+    greet_all(2, n)
+
+    def send(source, dst, core, chip, out_sem, in_sem):
+        itself = (core == a) & (chip == s)
+        copy = remote(source, dst, out_sem, in_sem, device_id=(core, chip))
+        return itself, copy, pltpu.make_async_copy(source, dst, in_sem)
+
+    def start(moves):
+        for itself, copy, here in moves:
+            pl.when(itself)(here.start)
+            pl.when(jnp.logical_not(itself))(copy.start)
+
+    def drain(moves):
+        for itself, copy, here in moves:
+            pl.when(jnp.logical_not(itself))(copy.wait_send)
+
+    def edges(i):
+        chip = h * a + i
+        yield send(packed.at[:, pl.ds(whole * i + whole - 1, 1)], held.at[s, :, 0:1], 0, lax.rem(chip + 1, n), edge_out.at[0, i], edge_in.at[s])
+        yield send(packed.at[:, pl.ds(whole * i, 1)], held.at[s, :, pairs + 1 : pairs + 2], 1, lax.rem(chip + n - 1, n), edge_out.at[1, i], edge_in.at[s])
+
+    def mains(i, m):
+        for core in range(2):
+            own = m if core == 0 else pairs - 1 - m
+            source = packed.at[:, pl.ds(whole * i + pairs * core + own, 1)]
+            yield send(source, held.at[s, :, own + 1 : own + 2], core, h * a + i, main_out.at[m, core, i], main_in.at[m, s])
+
+    @pl.loop(0, h)
+    def _(r):
+        start(edges(lax.rem(s + r, h)))
+
+    for m in range(pairs):
+        @pl.loop(0, h)
+        def _(r):
+            start(mains(lax.rem(s + r, h), m))
+
+    halos = [
+        remote(velocity, beside, halo_out.at[0], halo_in.at[0], device_id=(1 - a, s)),
+        remote(velocity.at[:, lp - 1], near.at[0], halo_out.at[1], halo_in.at[1], device_id=(a, lax.rem(s + 1, n))),
+        remote(velocity.at[:, 0], near.at[1], halo_out.at[2], halo_in.at[2], device_id=(a, lax.rem(s + n - 1, n))),
+    ]
+    for copy in halos:
+        copy.start()
+
+    column_weights((ny, lp, nx), inverse, block, bins, whi, wlo, onehot)
+    sums[...] = jnp.zeros(sums.shape, jnp.float32)
+
+    def slot_of(m):
+        return 1 + m + a * (pairs - 1 - 2 * m)
+
+    def forward(p):
+        return remote(
+            held.at[p, :, pl.ds(slot_of(pairs - 1), 1)], held.at[p, :, pl.ds((pairs + 1) * a, 1)],
+            pass_out.at[p], pass_in.at[p], device_id=(1 - a, s),
+        )
+
+    def await_pair(sems, p):
+        pltpu.make_async_copy(packed.at[:, 0:1], held.at[p, :, 0:1], sems).wait()
+
+    half = s // h
+    mine = 2 * lax.rem(s, h) + a
+
+    def returns(j, d):
+        pair = slot_of(j) - 1
+        return [send(back.at[j, d], home.at[mine, :, pair], half, d, back_out.at[j, d], back_in.at[j, mine])]
+
+    def column(j):
+        q = slot_of(j)
+        if j == 0:
+            field_columns(u, fields, 2 * q - 1, 4, nz, nx)
+        else:
+            field_columns(u, fields, 2 * q + 1 - 2 * a, 2, nz, nx)
+        filter_pair(fields, 2 * q - 1, high, low, filt, whi, wlo, nz)
+        stress_pair(filt, stress, sums, nz, nx)
+
+        @pl.loop(0, 6)
+        def _(f):
             rows = []
-            for hf in range(halves):
-                first = stress[f, hf, 2 * p * nz : (2 * p + 1) * nz, :]
-                second = stress[f, hf, (2 * p + 1) * nz : (2 * p + 2) * nz, :]
-                rows.extend(swap_bit(first, second, 4))
+            for hf in range(2):
+                rows.extend(swap_bit(stress[f, hf, 0:nz, :], stress[f, hf, nz : 2 * nz, :], 4))
             turned = jnp.concatenate(rows, axis=0).T
-            at = pl.ds(pl.multiple_of((f * pairs + p) * 8, 8), 8)
-            back[:, at, :] = turned.reshape(n, 8, nx)
+            back[j, :, f] = turned.reshape(n, 8, nx)
+
+        for r in range(n):
+            mask = (r % 2) * h + r // 2
+            start(returns(j, flip_bits(s, mask ^ h, bits)))
+
+    @pl.loop(0, n)
+    def _(p):
+        await_pair(edge_in.at[p], p)
+        await_pair(main_in.at[0, p], p)
+        await_pair(main_in.at[1, p], p)
+
+    for m in range(-1, 2):
+        unpack_pair(held, u, slot_of(m), nz, nx)
+    column(0)
+    for j in range(1, pairs):
+        if j + 1 < pairs:
+            @pl.loop(0, n)
+            def _(p):
+                await_pair(main_in.at[j + 1, p], p)
+                if j + 2 == pairs:
+                    forward(p).start()
+        else:
+            @pl.loop(0, n)
+            def _(p):
+                forward(p).wait()
+        unpack_pair(held, u, slot_of(j + 1), nz, nx)
+        column(j)
 
     exact = functools.partial(
         lax.dot_general, dimension_numbers=(((1,), (1,)), ((), ())),
@@ -367,85 +467,45 @@
     lm_bins = jnp.sum(exact(sums[0], onehot[...]), axis=0, keepdims=True) * (1.0 / 16.0)
     mm_bins = jnp.sum(exact(sums[1], onehot[...]), axis=0, keepdims=True) * (1.0 / 256.0)
     row = lax.broadcasted_iota(jnp.int32, (8, nx), 0)
-    tile = jnp.where(row < 4, lm_bins, mm_bins)
-    for p in range(n):
-        back[p, 6 * pairs * 8 :, :] = tile
-
-
-def gather_kernel(n, back, velocity, home, sums, out, beside, near, back_out, back_in, sum_out, sum_in, halo_out, halo_in):
-    _, lp, nz, nx = velocity.shape
-    a, s = lax.axis_index("px"), lax.axis_index("pz")
-    h = n // 2
-    rows = back.shape[1] - 8
-    greet_all(2, n)
-    slot = 2 * lax.rem(s, h) + a
-    half = s // h
-    remote = functools.partial(pltpu.make_async_remote_copy, device_id_type=MESH)
-    halos = [
-        remote(velocity, beside, halo_out.at[0], halo_in.at[0], device_id=(1 - a, s)),
-        remote(velocity.at[:, lp - 1], near.at[0], halo_out.at[1], halo_in.at[1], device_id=(a, lax.rem(s + 1, n))),
-        remote(velocity.at[:, 0], near.at[1], halo_out.at[2], halo_in.at[2], device_id=(a, lax.rem(s + n - 1, n))),
-    ]
-    for copy in halos:
-        copy.start()
-
-    def send(source, dst, core, chip, out_sem, in_sem):
-        itself = (core == a) & (chip == s)
-        copy = remote(source, dst, out_sem, in_sem, device_id=(core, chip))
-        return itself, copy, pltpu.make_async_copy(source, dst, in_sem)
-
-    def sends(p):
-        yield send(back.at[p], home.at[slot], half, p, back_out.at[p], back_in.at[slot])
-        yield send(back.at[p, pl.ds(rows, 8)], sums.at[slot], 1 - half, p, sum_out.at[p], sum_in.at[slot])
-
-    @pl.loop(0, n)
-    def _(i):
-        for itself, copy, here in sends(lax.rem(s + i, n)):
-            pl.when(itself)(here.start)
-            pl.when(jnp.logical_not(itself))(copy.start)
+    tile[...] = jnp.where(row < 4, lm_bins, mm_bins)
+    me = a * n + s
+
+    def share(t):
+        return [send(tile, totals.at[me], t // n, lax.rem(t, n), sum_out.at[t], sum_in.at[me])]
+
+    @pl.loop(0, 2 * n)
+    def _(r):
+        start(share(lax.rem(me + r, 2 * n)))
 
     for copy in halos:
         copy.wait()
-    lane = lax.broadcasted_iota(jnp.int32, (nz, nx), 1)
-    has_below = (s > 0).astype(jnp.float32)
-    has_above = (s < n - 1).astype(jnp.float32)
-
-    def plane(y, ups, downs):
-        dx, dy, dz = [], [], []
-        for c in range(3):
-            v, side = velocity[c, y], beside[c, y]
-            ahead = jnp.where(lane == nx - 1, pltpu.roll(side, nx - 1, 1), pltpu.roll(v, nx - 1, 1))
-            behind = jnp.where(lane == 0, pltpu.roll(side, 1, 1), pltpu.roll(v, 1, 1))
-            dx.append(ahead - behind)
-            dz.append(pltpu.roll(v, nz - 1, 0) - pltpu.roll(v, 1, 0))
-            dy.append(ups[c] - downs[c])
-        out[y] = tensor_norm(strain_of(dx, dy, dz))
-
-    line = [near[0, c] * has_below for c in range(3)]
-    plane(0, [velocity[c, 1] for c in range(3)], line)
-    line = [near[1, c] * has_above for c in range(3)]
-    plane(lp - 1, line, [velocity[c, lp - 2] for c in range(3)])
-
-    @pl.loop(1, lp - 1)
-    def _(y):
-        plane(y, [velocity[c, y + 1] for c in range(3)], [velocity[c, y - 1] for c in range(3)])
+    plane_magnitudes(velocity, beside, near, magnitude, (s > 0).astype(jnp.float32), (s < n - 1).astype(jnp.float32))
+
+    @pl.loop(0, h)
+    def _(i):
+        drain(edges(i))
+        for m in range(pairs):
+            drain(mains(i, m))
 
     @pl.loop(0, n)
     def _(p):
-        pltpu.make_async_copy(back.at[0], home.at[p], back_in.at[p]).wait()
-        pltpu.make_async_copy(back.at[0, pl.ds(rows, 8)], sums.at[p], sum_in.at[p]).wait()
-        for itself, copy, here in sends(p):
-            pl.when(jnp.logical_not(itself))(copy.wait_send)
+        for j in range(pairs):
+            pltpu.make_async_copy(back.at[0, 0], home.at[p, :, 0], back_in.at[j, p]).wait()
+            drain(returns(j, p))
+
+    @pl.loop(0, 2 * n)
+    def _(t):
+        pltpu.make_async_copy(tile, totals.at[t], sum_in.at[t]).wait()
+        drain(share(t))
 
 
 def finish_kernel(dims, cells, chip, home, sums, magnitude, bins, leonard, viscosity, coefficient):
     n, pairs, lp, nz, nx = dims
     ny, groups = n * lp, nx // nz
     steps = lp // groups
-    rows = 6 * pairs * 8
-    total = home[0, rows:, :] + sums[0]
-    for p in range(1, n):
-        total = total + (home[p, rows:, :] + sums[p])
+    total = sums[0]
+    for p in range(1, 2 * n):
+        total = total + sums[p]
     numer, denom = total[0:1, :], total[4:5, :]
     per_bin = numer / jnp.maximum(denom, jnp.float32(cells))
     exact = functools.partial(
@@ -485,7 +545,6 @@
     smem = pl.BlockSpec(memory_space=pltpu.SMEM)
     f32 = functools.partial(jax.ShapeDtypeStruct, dtype=jnp.float32)
     dma = pltpu.SemaphoreType.DMA
-    cells = 2 * pairs * nz
 
     packed = pl.pallas_call(
         functools.partial(pack_kernel, (lp, nz, nx)),
@@ -493,48 +552,46 @@
         in_specs=[vmem],
         out_specs=vmem,
     )(velocity)
-    held = pl.pallas_call(
-        functools.partial(spread_kernel, (n, h, pairs)),
-        out_shape=f32((n, 3, pairs + 2, 8, nx)),
-        in_specs=[vmem],
-        out_specs=vmem,
-        scratch_shapes=[dma((h, 2)), dma((h,)), dma((h,)), dma((n,)), dma((n,)), dma((n,)), dma((n,))],
-        compiler_params=pltpu.CompilerParams(collective_id=0, has_side_effects=True),
-    )(packed.reshape(3, nx * steps // 8, 8, nx))
-    back = pl.pallas_call(
-        functools.partial(strip_kernel, dims),
-        out_shape=f32((n, 6 * pairs * 8 + 8, nx)),
-        in_specs=[vmem] * 4,
-        out_specs=vmem,
+    room = functools.partial(pltpu.VMEM, dtype=jnp.float32)
+    home, sums, magnitude = pl.pallas_call(
+        functools.partial(flow_kernel, dims),
+        out_shape=(f32((n, 6, pairs, 8, nx)), f32((2 * n, 8, nx)), f32((lp, nz, nx))),
+        in_specs=[vmem] * 5,
+        out_specs=(vmem,) * 3,
         scratch_shapes=[
-            pltpu.VMEM((3, 2, 2 * pairs + 4, nz, nx), jnp.float32),
-            pltpu.VMEM((21, 2 * pairs + 2, 2, nz, nx), jnp.float32),
-            pltpu.VMEM((21, cells, ny), jnp.float32),
-            pltpu.VMEM((6, 2, cells, nx), jnp.float32),
+            room((n, 3, pairs + 2, 8, nx)),
+            room((3, 2, 2 * pairs + 4, nz, nx)),
+            room((21, 2 * pairs + 4, 2, nz, nx)),
+            pltpu.VMEM((21 * 2 * nz, ny), jnp.bfloat16),
+            pltpu.VMEM((21 * 2 * nz, ny), jnp.bfloat16),
+            room((21 * 2 * nz, ny)),
+            room((6, 2, 2 * nz, nx)),
+            room((pairs, n, 6, 8, nx)),
             pltpu.VMEM((ny, ny), jnp.bfloat16),
             pltpu.VMEM((ny, ny), jnp.bfloat16),
-            pltpu.VMEM((nx, ny), jnp.float32),
-            pltpu.VMEM((2, 8, ny), jnp.float32),
-        ],
-        compiler_params=pltpu.CompilerParams(vmem_limit_bytes=60 * 1024 * 1024),
-    )(held, filter_inverse, block, bins)
-    home, sums, magnitude = pl.pallas_call(
-        functools.partial(gather_kernel, n),
-        out_shape=(f32(back.shape), f32((n, 8, nx)), f32((lp, nz, nx))),
-        in_specs=[vmem] * 2,
-        out_specs=(vmem,) * 3,
-        scratch_shapes=[
-            pltpu.VMEM((3, lp, nz, nx), jnp.float32),
-            pltpu.VMEM((2, 3, nz, nx), jnp.float32),
+            room((nx, ny)),
+            room((2, 8, ny)),
+            room((8, nx)),
+            room((3, lp, nz, nx)),
+            room((2, 3, nz, nx)),
+            dma((pairs, 2, h)),
+            dma((2, h)),
+            dma((n,)),
+            dma((pairs, n)),
+            dma((2 * n,)),
+            dma((3,)),
+            dma((pairs, n)),
             dma((n,)),
             dma((n,)),
-            dma((n,)),
-            dma((n,)),
-            dma((3,)),
+            dma((pairs, n)),
+            dma((2 * n,)),
             dma((3,)),
         ],
-        compiler_params=pltpu.CompilerParams(collective_id=1, has_side_effects=True),
-    )(back, velocity)
+        compiler_params=pltpu.CompilerParams(
+            collective_id=0, has_side_effects=True, vmem_limit_bytes=60 * 1024 * 1024
+        ),
+    )(packed.reshape(3, nx * steps // 8, 8, nx), velocity, filter_inverse, block, bins)
+    home = home.reshape(n, 6 * pairs * 8, nx)
     leonard, viscosity, coefficient = pl.pallas_call(
         functools.partial(finish_kernel, dims, 2 * nx * nz),
         out_shape=(f32((6, lp, nz, nx)), f32((lp, nz, nx)), f32((1, ny))),

time: 105 us -> 83.5 us (0.80)
  the two profiles are of different devices: /device:TPU:15 before, /device:TPU:0 now
where the time goes in v2:
time: 83.5 us; the launch traced here: 83.3 us
  Pallas kernels  82.6 us (99%)
    pallas_call x1, Pallas kernels, by_strips(): pl.pallas_call(functools.partial(flow_kernel, dims), out_shape=(f32((n, 6...  75.3 us
    pallas_call x1, Pallas kernels, by_strips(): pl.pallas_call(functools.partial(finish_kernel, dims, 2 * nx * nz), out_s...  4.88 us
    pallas_call x1, Pallas kernels, by_strips(): pl.pallas_call(functools.partial(pack_kernel, (lp, nz, nx)), out_shape=f3...  2.42 us

profile of v2, /device:TPU:0, one launch (start us, length us, event | category | flops | bytes accessed | tf_op | source)
XLA Modules:
  0.0 83.3 jit_solution(8331433186213623915)
XLA Ops:
  0.6 2.4 %shard_map.67 = f32[3,512,128]{2,1,0:T(8,128)} custom-call(f32[3,16,32,128]{3,2,1,0:T(8,128)} %velocity.3), custom_call_target="tpu_custom_call" | custom-call | tf_op jit(solution)/shard_map/pallas_call | solution.py:549
  3.1 75.3 %shard_map.68 = (f32[16,6,4,8,128]{4,3,2,1,0:T(8,128)}, f32[32,8,128]{2,1,0:T(8,128)}, f32[16,32,128]{2,1,0:T(8,128)}) custom-call(f32[3,64,8,128]{3,2,1,0:T(8,128)} %bitcast.6, f32[3,16,32,128]{3,2,1,0:T(8,128)} %velocity.3, f32[256,256]{1,0:T(8,128)} %inverse.1, s32[1,256]{1,0:T(1,128)} %bitcast.10, s32[1,256]{1,0:T(1,128)} %bitcast.8), custom_call_target="tpu_custom_call" | custom-call | tf_op jit(solution)/shard_map/pallas_call | solution.py:556
  78.4 4.9 %shard_map.69 = (f32[6,16,32,128]{3,2,1,0:T(8,128)}, f32[16,32,128]{2,1,0:T(8,128)}, f32[1,256]{1,0:T(1,128)}) custom-call(s32[1]{0:T(128)} %bitcast.chip, f32[16,192,128]{2,1,0:T(8,128)} %bitcast.7, f32[32,8,128]{2,1,0:T(8,128)} %get-tuple-element.10.sums, f32[16,32,128]{2,1,0:T(8,128)} %get-tuple-element.11.magnitude, s32[1,256]{1,0:T(1,128)} %bitcast.9), custom_call_target="tpu_custom_call" | custom-call | tf_op jit(solution)/shard_map/pallas_call | solution.py:595

commit v3 on v2

--- a/solution.py
+++ b/solution.py
@@ -184,27 +184,29 @@
     return (at % nx) // 8 * lp + at // nx * 8 + at % 8
 
 
-def column_weights(dims, inverse, block, bins, whi, wlo, onehot):
+def column_weights(dims, upper, inverse, block, bins, wide, heavy, onehot):
     ny, lp, nx = dims
+    rows = ny // 2
     label = jnp.broadcast_to(block[...].astype(jnp.float32), (ny, ny))
-    masked = jnp.where(label == label.T, inverse[...], 0.0)
+    turned = label.T
+    mine = jnp.where(upper, turned[rows:], turned[:rows])
+    masked = jnp.where(label[:rows] == mine, jnp.where(upper, inverse[rows:, :], inverse[:rows, :]), 0.0)
     weights = masked / jnp.sum(masked, axis=1, keepdims=True) * 0.0625
     order = plane_order((ny, ny), lp, nx, 0) == lax.broadcasted_iota(jnp.int32, (ny, ny), 1)
     order = order.astype(jnp.float32).astype(jnp.bfloat16)
-    across = functools.partial(
-        lax.dot_general, dimension_numbers=(((1,), (1,)), ((), ())), preferred_element_type=jnp.float32
-    )
 
     def placed(part):
-        turned = across(order, part).astype(jnp.bfloat16)
-        return across(turned, order).astype(jnp.bfloat16)
-
-    heavy = weights.astype(jnp.bfloat16)
-    whi[...] = placed(heavy)
-    wlo[...] = placed((weights - heavy.astype(jnp.float32)).astype(jnp.bfloat16))
-    label = jnp.broadcast_to(bins[...], (nx, ny))
-    hot = (label == lax.broadcasted_iota(jnp.int32, (nx, ny), 0)).astype(jnp.float32)
-    onehot[...] = across(hot.astype(jnp.bfloat16), order)
+        dims = (((1,), (1,)), ((), ()))
+        return lax.dot_general(order, part, dims, preferred_element_type=jnp.float32).astype(jnp.bfloat16)
+
+    head = weights.astype(jnp.bfloat16)
+    rest = (weights - head.astype(jnp.float32)).astype(jnp.bfloat16)
+    heavy[...] = placed(head)
+    wide[:, :rows] = heavy[...]
+    wide[:, rows:] = placed(rest)
+    label = jnp.where(upper, bins[:, rows:], bins[:, :rows])
+    kind = lax.broadcasted_iota(jnp.int32, (nx, rows), 0)
+    onehot[...] = (jnp.broadcast_to(label, (nx, rows)) == kind).astype(jnp.float32)
 
 
 def flip_bits(value, mask, count):
@@ -241,8 +243,7 @@
 
 
 def unpack_pair(held, u, slot, nz, nx):
-    @pl.loop(0, 3)
-    def _(c):
+    for c in range(3):
         turned = held[:, c, slot].reshape(nx, nx).T
         for hf in range(2):
             first = turned[2 * hf * nz : (2 * hf + 1) * nz]
@@ -255,7 +256,7 @@
     last, first_lane = lane % 8 == 7, lane % 8 == 0
     top, bottom = lane == nx - 1, lane == 0
 
-    @pl.loop(0, count)
+    @pl.loop(0, count, unroll=2)
     def _(i):
         x = start + i
         here, dx, dy, dz = [], [], [], []
@@ -287,68 +288,70 @@
                 fields[15 + q, x, hf] = mag * s[q]
 
 
-def filter_pair(fields, start, high, low, filt, whi, wlo, nz):
+def filter_pair(fields, start, high, low, filt, wide, heavy, nz):
     cells = 2 * nz
 
-    @pl.loop(0, 21)
-    def _(k):
+    rows = wide.shape[1] // 2
+
+    def box(k):
         columns = []
         for hf in range(2):
             f = [fields[k, start + i, hf] for i in range(4)]
             pair = [f[i] + f[i + 1] for i in range(3)]
-            rows = []
+            parts = []
             for i in range(2):
                 along = pair[i] + pair[i + 1]
-                rows.append(pltpu.roll(along, 1, 0) + pltpu.roll(along, nz - 1, 0) + (along + along))
-            columns.append(jnp.concatenate(rows, axis=0))
-        box = jnp.concatenate(columns, axis=1)
-        heavy = box.astype(jnp.bfloat16)
-        at = pl.ds(pl.multiple_of(k * cells, cells), cells)
-        high[at, :] = heavy
-        low[at, :] = (box - heavy.astype(jnp.float32)).astype(jnp.bfloat16)
-
-    @pl.loop(0, 3)
-    def _(b):
-        dot = functools.partial(jnp.dot, preferred_element_type=jnp.float32)
-        at = pl.ds(pl.multiple_of(b * 7 * cells, cells), 7 * cells)
-        head, rest = high[at, :], low[at, :]
-        filt[at, :] = dot(head, whi[...]) + (dot(rest, whi[...]) + dot(head, wlo[...]))
-
-
-def stress_pair(filt, stress, sums, nz, nx):
+                parts.append(pltpu.roll(along, 1, 0) + pltpu.roll(along, nz - 1, 0) + (along + along))
+            columns.append(jnp.concatenate(parts, axis=0))
+        whole = jnp.concatenate(columns, axis=1)
+        head = whole.astype(jnp.bfloat16)
+        high[k * cells : (k + 1) * cells, :] = head
+        low[k * cells : (k + 1) * cells, :] = (whole - head.astype(jnp.float32)).astype(jnp.bfloat16)
+
+    dot = functools.partial(jnp.dot, preferred_element_type=jnp.float32)
+    for b in range(4):
+        if b < 3:
+            for k in range(7 * b, 7 * b + 7):
+                box(k)
+        if b:
+            at = slice((b - 1) * 7 * cells, b * 7 * cells)
+            both = dot(high[at, :], wide[...])
+            filt[at, :] = both[:, :rows] + (dot(low[at, :], heavy[...]) + both[:, rows:])
+
+
+def stress_pair(filt, stress, sums, place, nz):
     cells = 2 * nz
 
     @pl.loop(0, cells // 8)
     def _(r):
         base = pl.multiple_of(8 * r, 8)
-        for hf in range(2):
-            cols = slice(hf * nx, (hf + 1) * nx)
-            g = [filt[pl.ds(base + k * cells, 8), cols] for k in range(21)]
-            fmag = 4.0 * tensor_norm(g[3:9])
-            lm_total = jnp.zeros((8, nx), jnp.float32)
-            mm_total = jnp.zeros((8, nx), jnp.float32)
-            for q, (i, j) in enumerate(PAIRS):
-                leonard = g[9 + q] - g[i] * g[j]
-                model = g[15 + q] - fmag * g[3 + q]
-                weighted = model if q < 3 else 2.0 * model
-                lm_total += leonard * weighted
-                mm_total += model * weighted
-                stress[q, hf, pl.ds(base, 8), :] = leonard
-            sums[0, :, cols] += lm_total
-            sums[1, :, cols] += mm_total
+        g = [filt[pl.ds(base + k * cells, 8), :] for k in range(21)]
+        fmag = 4.0 * tensor_norm(g[3:9])
+        lm_total, mm_total = None, None
+        at = pl.ds(pl.multiple_of(place * cells + base, 8), 8)
+        for q, (i, j) in enumerate(PAIRS):
+            leonard = g[9 + q] - g[i] * g[j]
+            model = g[15 + q] - fmag * g[3 + q]
+            weighted = model if q < 3 else 2.0 * model
+            lm_total = leonard * weighted if q == 0 else lm_total + leonard * weighted
+            mm_total = model * weighted if q == 0 else mm_total + model * weighted
+            stress[q, at, :] = leonard
+        sums[0] += lm_total
+        sums[1] += mm_total
 
 
 def flow_kernel(
     dims, packed, velocity, inverse, block, bins, home, totals, magnitude,
-    held, u, fields, high, low, filt, stress, back, whi, wlo, onehot, sums, tile, beside, near,
+    held, u, fields, high, low, filt, stress, back, wide, heavy, onehot, sums, tile, beside, near,
     main_out, edge_out, pass_out, back_out, sum_out, halo_out,
     main_in, edge_in, pass_in, back_in, sum_in, halo_in,
 ):
     n, pairs, lp, nz, nx = dims
     ny, h = n * lp, n // 2
-    bits = n.bit_length() - 1
+    strips = h // 2
     whole = 2 * pairs
     a, s = lax.axis_index("px"), lax.axis_index("pz")
+    half, spot = s // h, lax.rem(s, h)
     remote = functools.partial(pltpu.make_async_remote_copy, device_id_type=MESH)
     greet_all(2, n)
 
@@ -366,25 +369,24 @@
         for itself, copy, here in moves:
             pl.when(jnp.logical_not(itself))(copy.wait_send)
 
-    def edges(i):
-        chip = h * a + i
-        yield send(packed.at[:, pl.ds(whole * i + whole - 1, 1)], held.at[s, :, 0:1], 0, lax.rem(chip + 1, n), edge_out.at[0, i], edge_in.at[s])
-        yield send(packed.at[:, pl.ds(whole * i, 1)], held.at[s, :, pairs + 1 : pairs + 2], 1, lax.rem(chip + n - 1, n), edge_out.at[1, i], edge_in.at[s])
-
-    def mains(i, m):
+    def edges(r):
+        t, i = r // strips, lax.rem(r, strips)
+        strip = strips * a + i
+        left = packed.at[:, pl.ds(whole * i + whole - 1, 1)]
+        yield send(left, held.at[s, :, 0:1], 0, h * t + lax.rem(strip + 1, h), edge_out.at[0, r], edge_in.at[s])
+        right = packed.at[:, pl.ds(whole * i, 1)]
+        yield send(right, held.at[s, :, pairs + 1 : pairs + 2], 1, h * t + lax.rem(strip + h - 1, h), edge_out.at[1, r], edge_in.at[s])
+
+    def mains(r, m):
+        t, i = r // strips, lax.rem(r, strips)
         for core in range(2):
-            own = m if core == 0 else pairs - 1 - m
+            own = m if core else pairs - 1 - m
             source = packed.at[:, pl.ds(whole * i + pairs * core + own, 1)]
-            yield send(source, held.at[s, :, own + 1 : own + 2], core, h * a + i, main_out.at[m, core, i], main_in.at[m, s])
-
-    @pl.loop(0, h)
-    def _(r):
-        start(edges(lax.rem(s + r, h)))
-
-    for m in range(pairs):
-        @pl.loop(0, h)
-        def _(r):
-            start(mains(lax.rem(s + r, h), m))
+            dst = held.at[s, :, pl.ds(own + 1, 1)]
+            yield send(source, dst, core, h * t + strips * a + i, main_out.at[m, core, r], main_in.at[m, s])
+
+    def ordered(r):
+        return lax.rem(half + 1 + r // strips, 2) * strips + lax.rem(s + r, strips)
 
     halos = [
         remote(velocity, beside, halo_out.at[0], halo_in.at[0], device_id=(1 - a, s)),
@@ -394,71 +396,97 @@
     for copy in halos:
         copy.start()
 
-    column_weights((ny, lp, nx), inverse, block, bins, whi, wlo, onehot)
+    @pl.loop(0, pairs)
+    def _(m):
+        @pl.loop(0, h)
+        def _(r):
+            start(mains(ordered(r), m))
+
+    @pl.loop(0, h)
+    def _(r):
+        start(edges(ordered(r)))
+
+    column_weights((ny, lp, nx), half == 1, inverse, block, bins, wide, heavy, onehot)
     sums[...] = jnp.zeros(sums.shape, jnp.float32)
 
     def slot_of(m):
-        return 1 + m + a * (pairs - 1 - 2 * m)
+        return pairs - m + a * (1 + 2 * m - pairs)
 
     def forward(p):
         return remote(
-            held.at[p, :, pl.ds(slot_of(pairs - 1), 1)], held.at[p, :, pl.ds((pairs + 1) * a, 1)],
+            held.at[p, :, pl.ds(slot_of(0), 1)], held.at[p, :, pl.ds((pairs + 1) * a, 1)],
             pass_out.at[p], pass_in.at[p], device_id=(1 - a, s),
         )
 
-    def await_pair(sems, p):
-        pltpu.make_async_copy(packed.at[:, 0:1], held.at[p, :, 0:1], sems).wait()
-
-    half = s // h
-    mine = 2 * lax.rem(s, h) + a
+    def await_pair(sem, p):
+        pltpu.make_async_copy(packed.at[:, 0:1], held.at[p, :, 0:1], sem).wait()
+
+    mine = 2 * lax.rem(spot, strips) + a
 
     def returns(j, d):
-        pair = slot_of(j) - 1
-        return [send(back.at[j, d], home.at[mine, :, pair], half, d, back_out.at[j, d], back_in.at[j, mine])]
-
-    def column(j):
-        q = slot_of(j)
-        if j == 0:
-            field_columns(u, fields, 2 * q - 1, 4, nz, nx)
-        else:
-            field_columns(u, fields, 2 * q + 1 - 2 * a, 2, nz, nx)
-        filter_pair(fields, 2 * q - 1, high, low, filt, whi, wlo, nz)
-        stress_pair(filt, stress, sums, nz, nx)
-
+        place = pairs // 2 - 1 - j + a * (1 + 2 * j - pairs // 2)
+        source, dst = back.at[j, d], home.at[mine, :, place]
+        return [send(source, dst, spot // strips, h * half + d, back_out.at[j, d], back_in.at[j, mine])]
+
+    def column(m, count):
+        q = slot_of(m)
+        field_columns(u, fields, 2 * q - 1 if count == 4 else 2 * q - 1 + 2 * a, count, nz, nx)
+        filter_pair(fields, 2 * q - 1, high, low, filt, wide, heavy, nz)
+        stress_pair(filt, stress, sums, lax.rem(q - 1, 2), nz)
+
+    def give_back(j):
         @pl.loop(0, 6)
         def _(f):
-            rows = []
-            for hf in range(2):
-                rows.extend(swap_bit(stress[f, hf, 0:nz, :], stress[f, hf, nz : 2 * nz, :], 4))
-            turned = jnp.concatenate(rows, axis=0).T
-            back[j, :, f] = turned.reshape(n, 8, nx)
-
-        for r in range(n):
-            mask = (r % 2) * h + r // 2
-            start(returns(j, flip_bits(s, mask ^ h, bits)))
+            rows = [stress[f, x * nz : (x + 1) * nz, :] for x in range(4)]
+            rows[0], rows[1] = swap_bit(rows[0], rows[1], 4)
+            rows[2], rows[3] = swap_bit(rows[2], rows[3], 4)
+            rows[0], rows[2] = swap_bit(rows[0], rows[2], 8)
+            rows[1], rows[3] = swap_bit(rows[1], rows[3], 8)
+            back[j, :, f] = jnp.concatenate(rows, axis=0).T.reshape(h, lp, nx)
+
+        for r in range(h):
+            start(returns(j, flip_bits(spot, h - 1 - r, h.bit_length() - 1)))
+
+    for copy in halos:
+        copy.wait()
+    plane_magnitudes(velocity, beside, near, magnitude, (s > 0).astype(jnp.float32), (s < n - 1).astype(jnp.float32))
 
     @pl.loop(0, n)
     def _(p):
-        await_pair(edge_in.at[p], p)
         await_pair(main_in.at[0, p], p)
+        forward(p).start()
+
+    unpack_pair(held, u, slot_of(0), nz, nx)
+
+    @pl.loop(0, n)
+    def _(p):
+        forward(p).wait()
         await_pair(main_in.at[1, p], p)
 
-    for m in range(-1, 2):
-        unpack_pair(held, u, slot_of(m), nz, nx)
-    column(0)
-    for j in range(1, pairs):
-        if j + 1 < pairs:
+    unpack_pair(held, u, slot_of(-1), nz, nx)
+    unpack_pair(held, u, slot_of(1), nz, nx)
+    column(0, 4)
+
+    @pl.loop(1, pairs)
+    def _(m):
+        @pl.when(m < pairs - 1)
+        def _():
             @pl.loop(0, n)
             def _(p):
-                await_pair(main_in.at[j + 1, p], p)
-                if j + 2 == pairs:
-                    forward(p).start()
-        else:
+                await_pair(main_in.at[m + 1, p], p)
+
+        @pl.when(m == pairs - 1)
+        def _():
             @pl.loop(0, n)
             def _(p):
-                forward(p).wait()
-        unpack_pair(held, u, slot_of(j + 1), nz, nx)
-        column(j)
+                await_pair(edge_in.at[p], p)
+
+        unpack_pair(held, u, slot_of(m + 1), nz, nx)
+        column(m, 2)
+
+        @pl.when(lax.rem(m, 2) == 1)
+        def _():
+            give_back(m // 2)
 
     exact = functools.partial(
         lax.dot_general, dimension_numbers=(((1,), (1,)), ((), ())),
@@ -477,19 +505,17 @@
     def _(r):
         start(share(lax.rem(me + r, 2 * n)))
 
-    for copy in halos:
-        copy.wait()
-    plane_magnitudes(velocity, beside, near, magnitude, (s > 0).astype(jnp.float32), (s < n - 1).astype(jnp.float32))
-
     @pl.loop(0, h)
-    def _(i):
-        drain(edges(i))
-        for m in range(pairs):
-            drain(mains(i, m))
-
-    @pl.loop(0, n)
+    def _(r):
+        drain(edges(r))
+
+        @pl.loop(0, pairs)
+        def _(m):
+            drain(mains(r, m))
+
+    @pl.loop(0, h)
     def _(p):
-        for j in range(pairs):
+        for j in range(pairs // 2):
             pltpu.make_async_copy(back.at[0, 0], home.at[p, :, 0], back_in.at[j, p]).wait()
             drain(returns(j, p))
 
@@ -526,8 +552,8 @@
     @pl.loop(0, 6)
     def _(f):
         for q in range(steps):
-            at = pl.ds(f * pairs * 8 + q, nx // n, stride=steps)
-            turned = jnp.concatenate([home[p, at, :] for p in range(n)], axis=0).T
+            at = pl.ds(f * pairs * 8 + q, 2 * pairs, stride=steps)
+            turned = jnp.concatenate([home[p, at, :] for p in range(nx // (2 * pairs))], axis=0).T
             for g in range(groups):
                 leonard[f, g * steps + q] = turned[g * nz : (g + 1) * nz]
 
@@ -535,7 +561,7 @@
 def by_strips(velocity, filter_inverse, filter_block, plane_bin, n):
     _, lp, nz, nx = velocity.shape
     ny, h = n * lp, n // 2
-    pairs = nx // h // 4
+    pairs = nx // h // 2
     dims = (n, pairs, lp, nz, nx)
     steps = lp // (nx // nz)
     chip = lax.axis_index("pz").astype(jnp.int32).reshape(1)
@@ -555,7 +581,7 @@
     room = functools.partial(pltpu.VMEM, dtype=jnp.float32)
     home, sums, magnitude = pl.pallas_call(
         functools.partial(flow_kernel, dims),
-        out_shape=(f32((n, 6, pairs, 8, nx)), f32((2 * n, 8, nx)), f32((lp, nz, nx))),
+        out_shape=(f32((h, 6, pairs // 2, lp, nx)), f32((2 * n, 8, nx)), f32((lp, nz, nx))),
         in_specs=[vmem] * 5,
         out_specs=(vmem,) * 3,
         scratch_shapes=[
@@ -564,26 +590,26 @@
             room((21, 2 * pairs + 4, 2, nz, nx)),
             pltpu.VMEM((21 * 2 * nz, ny), jnp.bfloat16),
             pltpu.VMEM((21 * 2 * nz, ny), jnp.bfloat16),
-            room((21 * 2 * nz, ny)),
-            room((6, 2, 2 * nz, nx)),
-            room((pairs, n, 6, 8, nx)),
+            room((21 * 2 * nz, ny // 2)),
+            room((6, 4 * nz, nx)),
+            room((pairs // 2, h, 6, lp, nx)),
             pltpu.VMEM((ny, ny), jnp.bfloat16),
-            pltpu.VMEM((ny, ny), jnp.bfloat16),
-            room((nx, ny)),
-            room((2, 8, ny)),
+            pltpu.VMEM((ny, ny // 2), jnp.bfloat16),
+            room((nx, ny // 2)),
+            room((2, 8, ny // 2)),
             room((8, nx)),
             room((3, lp, nz, nx)),
             room((2, 3, nz, nx)),
             dma((pairs, 2, h)),
             dma((2, h)),
             dma((n,)),
-            dma((pairs, n)),
+            dma((pairs // 2, h)),
             dma((2 * n,)),
             dma((3,)),
             dma((pairs, n)),
             dma((n,)),
             dma((n,)),
-            dma((pairs, n)),
+            dma((pairs // 2, h)),
             dma((2 * n,)),
             dma((3,)),
         ],
@@ -591,7 +617,7 @@
             collective_id=0, has_side_effects=True, vmem_limit_bytes=60 * 1024 * 1024
         ),
     )(packed.reshape(3, nx * steps // 8, 8, nx), velocity, filter_inverse, block, bins)
-    home = home.reshape(n, 6 * pairs * 8, nx)
+    home = home.reshape(h, 6 * pairs // 2 * lp, nx)
     leonard, viscosity, coefficient = pl.pallas_call(
         functools.partial(finish_kernel, dims, 2 * nx * nz),
         out_shape=(f32((6, lp, nz, nx)), f32((lp, nz, nx)), f32((1, ny))),
@@ -666,7 +692,7 @@
     _, lp, nz, nx = arrays[0].shape
     n, m = lax.axis_size("pz"), lax.axis_size("px")
     groups = nx // nz
-    fits = m == 2 and n % 2 == 0 and 8 * n == nx and groups * nz == nx and lp == 16 and groups == 4
+    fits = m == 2 and n % 4 == 0 and 8 * n == nx and groups * nz == nx and lp == 16 and groups == 4
     if fits:
         return by_strips(*arrays, n)
     return by_blocks(*arrays)

time: 83.5 us -> 76.2 us (0.913)
  Pallas kernels: 82.6 us -> 75.4 us
    pallas_call x1, Pallas kernels: 75.3 us -> 68.1 us  [by_strips(): pl.pallas_call(functools.partial(flow_kernel, dims), out_shape=(f32((h, 6...]
where the time goes in v3:
time: 76.2 us; the launch traced here: 76 us
  Pallas kernels  75.4 us (99%)
    pallas_call x1, Pallas kernels, by_strips(): pl.pallas_call(functools.partial(flow_kernel, dims), out_shape=(f32((h, 6...  68.1 us
    pallas_call x1, Pallas kernels, by_strips(): pl.pallas_call(functools.partial(finish_kernel, dims, 2 * nx * nz), out_s...  4.88 us
    pallas_call x1, Pallas kernels, by_strips(): pl.pallas_call(functools.partial(pack_kernel, (lp, nz, nx)), out_shape=f3...  2.42 us

profile of v3, /device:TPU:0, one launch (start us, length us, event | category | flops | bytes accessed | tf_op | source)
XLA Modules:
  0.0 76.0 jit_solution(8611211106316811625)
XLA Ops:
  0.6 2.4 %shard_map.67 = f32[3,512,128]{2,1,0:T(8,128)} custom-call(f32[3,16,32,128]{3,2,1,0:T(8,128)} %velocity.3), custom_call_target="tpu_custom_call" | custom-call | tf_op jit(solution)/shard_map/pallas_call | solution.py:575
  3.1 68.1 %shard_map.68 = (f32[8,6,4,16,128]{4,3,2,1,0:T(8,128)}, f32[32,8,128]{2,1,0:T(8,128)}, f32[16,32,128]{2,1,0:T(8,128)}) custom-call(f32[3,64,8,128]{3,2,1,0:T(8,128)} %bitcast.6, f32[3,16,32,128]{3,2,1,0:T(8,128)} %velocity.3, f32[256,256]{1,0:T(8,128)} %inverse.1, s32[1,256]{1,0:T(1,128)} %bitcast.10, s32[1,256]{1,0:T(1,128)} %bitcast.8), custom_call_target="tpu_custom_call" | custom-call | tf_op jit(solution)/shard_map/pallas_call | solution.py:582
  71.1 4.9 %shard_map.69 = (f32[6,16,32,128]{3,2,1,0:T(8,128)}, f32[16,32,128]{2,1,0:T(8,128)}, f32[1,256]{1,0:T(1,128)}) custom-call(s32[1]{0:T(128)} %bitcast.chip, f32[8,384,128]{2,1,0:T(8,128)} %bitcast.7, f32[32,8,128]{2,1,0:T(8,128)} %get-tuple-element.10.sums, f32[16,32,128]{2,1,0:T(8,128)} %get-tuple-element.11.magnitude, s32[1,256]{1,0:T(1,128)} %bitcast.9), custom_call_target="tpu_custom_call" | custom-call | tf_op jit(solution)/shard_map/pallas_call | solution.py:621

commit v4 on v3

--- a/solution.py
+++ b/solution.py
@@ -167,13 +167,11 @@
     )
 
 
-def pack_kernel(dims, velocity, packed):
-    lp, nz, nx = dims
+def pack_planes(velocity, packed):
+    _, lp, nz, nx = velocity.shape
     groups = nx // nz
     steps = lp // groups
-
-    @pl.loop(0, 3)
-    def _(c):
+    for c in range(3):
         for q in range(steps):
             rows = jnp.concatenate([velocity[c, g * steps + q] for g in range(groups)], axis=0)
             packed[c, pl.ds(q, nx, stride=steps), :] = rows.T
@@ -341,8 +339,8 @@
 
 
 def flow_kernel(
-    dims, packed, velocity, inverse, block, bins, home, totals, magnitude,
-    held, u, fields, high, low, filt, stress, back, wide, heavy, onehot, sums, tile, beside, near,
+    dims, velocity, inverse, block, bins, home, totals, magnitude,
+    packed, held, u, fields, high, low, filt, stress, back, wide, heavy, onehot, sums, tile, beside, near,
     main_out, edge_out, pass_out, back_out, sum_out, halo_out,
     main_in, edge_in, pass_in, back_in, sum_in, halo_in,
 ):
@@ -353,7 +351,16 @@
     a, s = lax.axis_index("px"), lax.axis_index("pz")
     half, spot = s // h, lax.rem(s, h)
     remote = functools.partial(pltpu.make_async_remote_copy, device_id_type=MESH)
-    greet_all(2, n)
+    barrier = pltpu.get_barrier_semaphore()
+    me = a * n + s
+
+    @pl.loop(1, 2 * n)
+    def _(step):
+        peer = lax.rem(me + step, 2 * n)
+        pl.semaphore_signal(barrier, inc=1, device_id=(peer // n, lax.rem(peer, n)), device_id_type=MESH)
+
+    pack_planes(velocity, packed)
+    pl.semaphore_wait(barrier, 2 * n - 1)
 
     def send(source, dst, core, chip, out_sem, in_sem):
         itself = (core == a) & (chip == s)
@@ -369,21 +376,22 @@
         for itself, copy, here in moves:
             pl.when(jnp.logical_not(itself))(copy.wait_send)
 
+    def piece(pair):
+        return packed.at[:, pl.ds(pl.multiple_of(8 * pair, 8), 8)]
+
     def edges(r):
         t, i = r // strips, lax.rem(r, strips)
-        strip = strips * a + i
-        left = packed.at[:, pl.ds(whole * i + whole - 1, 1)]
-        yield send(left, held.at[s, :, 0:1], 0, h * t + lax.rem(strip + 1, h), edge_out.at[0, r], edge_in.at[s])
-        right = packed.at[:, pl.ds(whole * i, 1)]
-        yield send(right, held.at[s, :, pairs + 1 : pairs + 2], 1, h * t + lax.rem(strip + h - 1, h), edge_out.at[1, r], edge_in.at[s])
+        after = h * t + lax.rem(strips * a + i + 1, h)
+        before = h * t + lax.rem(strips * a + i + h - 1, h)
+        yield send(piece(whole * i + whole - 1), held.at[s, :, 0], 0, after, edge_out.at[0, r], edge_in.at[s])
+        yield send(piece(whole * i), held.at[s, :, pairs + 1], 1, before, edge_out.at[1, r], edge_in.at[s])
 
     def mains(r, m):
         t, i = r // strips, lax.rem(r, strips)
         for core in range(2):
             own = m if core else pairs - 1 - m
-            source = packed.at[:, pl.ds(whole * i + pairs * core + own, 1)]
-            dst = held.at[s, :, pl.ds(own + 1, 1)]
-            yield send(source, dst, core, h * t + strips * a + i, main_out.at[m, core, r], main_in.at[m, s])
+            dst = held.at[s, :, own + 1]
+            yield send(piece(whole * i + pairs * core + own), dst, core, h * t + strips * a + i, main_out.at[m, core, r], main_in.at[m, s])
 
     def ordered(r):
         return lax.rem(half + 1 + r // strips, 2) * strips + lax.rem(s + r, strips)
@@ -414,12 +422,12 @@
 
     def forward(p):
         return remote(
-            held.at[p, :, pl.ds(slot_of(0), 1)], held.at[p, :, pl.ds((pairs + 1) * a, 1)],
+            held.at[p, :, slot_of(0)], held.at[p, :, (pairs + 1) * a],
             pass_out.at[p], pass_in.at[p], device_id=(1 - a, s),
         )
 
     def await_pair(sem, p):
-        pltpu.make_async_copy(packed.at[:, 0:1], held.at[p, :, 0:1], sem).wait()
+        pltpu.make_async_copy(packed.at[:, 0:8], held.at[p, :, 0], sem).wait()
 
     mine = 2 * lax.rem(spot, strips) + a
 
@@ -484,7 +492,7 @@
         unpack_pair(held, u, slot_of(m + 1), nz, nx)
         column(m, 2)
 
-        @pl.when(lax.rem(m, 2) == 1)
+        @pl.when((lax.rem(m, 2) == 1) & (m < pairs - 1))
         def _():
             give_back(m // 2)
 
@@ -492,11 +500,9 @@
         lax.dot_general, dimension_numbers=(((1,), (1,)), ((), ())),
         preferred_element_type=jnp.float32, precision=lax.Precision.HIGHEST,
     )
-    lm_bins = jnp.sum(exact(sums[0], onehot[...]), axis=0, keepdims=True) * (1.0 / 16.0)
-    mm_bins = jnp.sum(exact(sums[1], onehot[...]), axis=0, keepdims=True) * (1.0 / 256.0)
-    row = lax.broadcasted_iota(jnp.int32, (8, nx), 0)
-    tile[...] = jnp.where(row < 4, lm_bins, mm_bins)
-    me = a * n + s
+    spread = exact(sums[...].reshape(16, nx), onehot[...])
+    tile[0:1, :] = jnp.sum(spread[0:8], axis=0, keepdims=True) * (1.0 / 16.0)
+    tile[1:2, :] = jnp.sum(spread[8:16], axis=0, keepdims=True) * (1.0 / 256.0)
 
     def share(t):
         return [send(tile, totals.at[me], t // n, lax.rem(t, n), sum_out.at[t], sum_in.at[me])]
@@ -504,6 +510,8 @@
     @pl.loop(0, 2 * n)
     def _(r):
         start(share(lax.rem(me + r, 2 * n)))
+
+    give_back(pairs // 2 - 1)
 
     @pl.loop(0, h)
     def _(r):
@@ -532,7 +540,7 @@
     total = sums[0]
     for p in range(1, 2 * n):
         total = total + sums[p]
-    numer, denom = total[0:1, :], total[4:5, :]
+    numer, denom = total[0:1, :], total[1:2, :]
     per_bin = numer / jnp.maximum(denom, jnp.float32(cells))
     exact = functools.partial(
         lax.dot_general, preferred_element_type=jnp.float32, precision=lax.Precision.HIGHEST
@@ -549,8 +557,7 @@
     for y in range(lp):
         viscosity[y] = spread[y : y + 1, :] * magnitude[y]
 
-    @pl.loop(0, 6)
-    def _(f):
+    for f in range(6):
         for q in range(steps):
             at = pl.ds(f * pairs * 8 + q, 2 * pairs, stride=steps)
             turned = jnp.concatenate([home[p, at, :] for p in range(nx // (2 * pairs))], axis=0).T
@@ -572,19 +579,14 @@
     f32 = functools.partial(jax.ShapeDtypeStruct, dtype=jnp.float32)
     dma = pltpu.SemaphoreType.DMA
 
-    packed = pl.pallas_call(
-        functools.partial(pack_kernel, (lp, nz, nx)),
-        out_shape=f32((3, nx * steps, nx)),
-        in_specs=[vmem],
-        out_specs=vmem,
-    )(velocity)
     room = functools.partial(pltpu.VMEM, dtype=jnp.float32)
     home, sums, magnitude = pl.pallas_call(
         functools.partial(flow_kernel, dims),
-        out_shape=(f32((h, 6, pairs // 2, lp, nx)), f32((2 * n, 8, nx)), f32((lp, nz, nx))),
-        in_specs=[vmem] * 5,
+        out_shape=(f32((h, 6, pairs // 2, lp, nx)), f32((2 * n, 2, nx)), f32((lp, nz, nx))),
+        in_specs=[vmem] * 4,
         out_specs=(vmem,) * 3,
         scratch_shapes=[
+            room((3, nx * steps, nx)),
             room((n, 3, pairs + 2, 8, nx)),
             room((3, 2, 2 * pairs + 4, nz, nx)),
             room((21, 2 * pairs + 4, 2, nz, nx)),
@@ -597,7 +599,7 @@
             pltpu.VMEM((ny, ny // 2), jnp.bfloat16),
             room((nx, ny // 2)),
             room((2, 8, ny // 2)),
-            room((8, nx)),
+            room((2, nx)),
             room((3, lp, nz, nx)),
             room((2, 3, nz, nx)),
             dma((pairs, 2, h)),
@@ -616,7 +618,7 @@
         compiler_params=pltpu.CompilerParams(
             collective_id=0, has_side_effects=True, vmem_limit_bytes=60 * 1024 * 1024
         ),
-    )(packed.reshape(3, nx * steps // 8, 8, nx), velocity, filter_inverse, block, bins)
+    )(velocity, filter_inverse, block, bins)
     home = home.reshape(h, 6 * pairs // 2 * lp, nx)
     leonard, viscosity, coefficient = pl.pallas_call(
         functools.partial(finish_kernel, dims, 2 * nx * nz),

time: 76.2 us -> 71.3 us (0.936)
  Pallas kernels: 75.4 us -> 70.5 us
    pallas_call x1 -> x0, Pallas kernels: 2.42 us -> none  [by_strips(): pl.pallas_call(functools.partial(pack_kernel, (lp, nz, nx)), out_shape=f3...]
    pallas_call x1, Pallas kernels: 68.1 us -> 66.2 us  [by_strips(): pl.pallas_call(functools.partial(flow_kernel, dims), out_shape=(f32((h, 6...]
where the time goes in v4:
time: 71.3 us; the launch traced here: 71.1 us
  Pallas kernels  70.5 us (99%)
    pallas_call x1, Pallas kernels, by_strips(): pl.pallas_call(functools.partial(flow_kernel, dims), out_shape=(f32((h, 6...  66.2 us
    pallas_call x1, Pallas kernels, by_strips(): pl.pallas_call(functools.partial(finish_kernel, dims, 2 * nx * nz), out_s...  4.23 us

profile of v4, /device:TPU:0, one launch (start us, length us, event | category | flops | bytes accessed | tf_op | source)
XLA Modules:
  0.0 71.1 jit_solution(16005968991278621728)
XLA Ops:
  0.6 66.2 %shard_map.67 = (f32[8,6,4,16,128]{4,3,2,1,0:T(8,128)}, f32[32,2,128]{2,1,0:T(2,128)}, f32[16,32,128]{2,1,0:T(8,128)}) custom-call(f32[3,16,32,128]{3,2,1,0:T(8,128)} %velocity.1, f32[256,256]{1,0:T(8,128)} %inverse.1, s32[1,256]{1,0:T(1,128)} %bitcast.8, s32[1,256]{1,0:T(1,128)} %bitcast.6), custom_call_target="tpu_custom_call" | custom-call | tf_op jit(solution)/shard_map/pallas_call | solution.py:583
  66.9 4.2 %shard_map.68 = (f32[6,16,32,128]{3,2,1,0:T(8,128)}, f32[16,32,128]{2,1,0:T(8,128)}, f32[1,256]{1,0:T(1,128)}) custom-call(s32[1]{0:T(128)} %bitcast.chip, f32[8,384,128]{2,1,0:T(8,128)} %bitcast.5, f32[32,2,128]{2,1,0:T(2,128)} %get-tuple-element.10.sums, f32[16,32,128]{2,1,0:T(8,128)} %get-tuple-element.11.magnitude, s32[1,256]{1,0:T(1,128)} %bitcast.7), custom_call_target="tpu_custom_call" | custom-call | tf_op jit(solution)/shard_map/pallas_call | solution.py:623

commit v5 on v4

--- a/solution.py
+++ b/solution.py
@@ -443,8 +443,7 @@
         stress_pair(filt, stress, sums, lax.rem(q - 1, 2), nz)
 
     def give_back(j):
-        @pl.loop(0, 6)
-        def _(f):
+        for f in range(6):
             rows = [stress[f, x * nz : (x + 1) * nz, :] for x in range(4)]
             rows[0], rows[1] = swap_bit(rows[0], rows[1], 4)
             rows[2], rows[3] = swap_bit(rows[2], rows[3], 4)

time: 71.3 us -> 70.7 us (level); the launches traced: 71.1 us -> 69.6 us
  Pallas kernels: 70.5 us -> 69 us
    pallas_call x1, Pallas kernels: 66.2 us -> 64.7 us  [by_strips(): pl.pallas_call(functools.partial(flow_kernel, dims), out_shape=(f32((h, 6...]
where the time goes in v5:
time: 70.7 us; the launch traced here: 69.6 us
  Pallas kernels  69 us (98%)
    pallas_call x1, Pallas kernels, by_strips(): pl.pallas_call(functools.partial(flow_kernel, dims), out_shape=(f32((h, 6...  64.7 us
    pallas_call x1, Pallas kernels, by_strips(): pl.pallas_call(functools.partial(finish_kernel, dims, 2 * nx * nz), out_s...  4.23 us

profile of v5, /device:TPU:0, one launch (start us, length us, event | category | flops | bytes accessed | tf_op | source)
XLA Modules:
  0.0 69.6 jit_solution(6776362048992471166)
XLA Ops:
  0.6 64.7 %shard_map.67 = (f32[8,6,4,16,128]{4,3,2,1,0:T(8,128)}, f32[32,2,128]{2,1,0:T(2,128)}, f32[16,32,128]{2,1,0:T(8,128)}) custom-call(f32[3,16,32,128]{3,2,1,0:T(8,128)} %velocity.1, f32[256,256]{1,0:T(8,128)} %inverse.1, s32[1,256]{1,0:T(1,128)} %bitcast.8, s32[1,256]{1,0:T(1,128)} %bitcast.6), custom_call_target="tpu_custom_call" | custom-call | tf_op jit(solution)/shard_map/pallas_call | solution.py:582
  65.4 4.2 %shard_map.68 = (f32[6,16,32,128]{3,2,1,0:T(8,128)}, f32[16,32,128]{2,1,0:T(8,128)}, f32[1,256]{1,0:T(1,128)}) custom-call(s32[1]{0:T(128)} %bitcast.chip, f32[8,384,128]{2,1,0:T(8,128)} %bitcast.5, f32[32,2,128]{2,1,0:T(2,128)} %get-tuple-element.10.sums, f32[16,32,128]{2,1,0:T(8,128)} %get-tuple-element.11.magnitude, s32[1,256]{1,0:T(1,128)} %bitcast.7), custom_call_target="tpu_custom_call" | custom-call | tf_op jit(solution)/shard_map/pallas_call | solution.py:622
